TPU v7x, 128 devices: a whole 4x4x4 slice. The times are simulated.
128 devices in a mesh: dp: 8 (over x, core), crop: 4 (over y), tensor: 4 (over z).
Axes of the slice: x: 4, y: 4, z: 4, core: 2. Of those that a mesh axis runs over, the one named last changes fastest.
Arguments:
- hidden_a: bfloat16 [2048, 8192], P('crop', 'dp'), as said below
- hidden_b: bfloat16 [2048, 8192], P('crop', 'dp'), as said below
- weight: bfloat16 [8192, 8192], P('dp', 'tensor')
Outputs:
- weight_grad: float32 [8192, 8192], P(('dp', 'crop'), 'tensor')
Inputs may be any that keep to these rules, and one draw needn't show every extreme that they name: `hidden_a`: nonnegative entries. `hidden_b`: nonnegative entries.
All inputs are finite; a program needn't handle non-finite values.
Results may differ from a plain program's by a relative error of at most 0.0015.
Values may be sent and summed in bfloat16 or wider, within the bound.
No kernel may reach another device: no remote copies, remote signals or barrier semaphores. Data moves between devices by JAX's collectives and lax.ppermute only.
A program may use at most 128 MiB of HBM per device.

v0:
```python
import jax
import jax.numpy as jnp
from jax import lax
from jax.sharding import Mesh
from jax.sharding import PartitionSpec as P

epsilon = 0.0001
others = (1, -1, 2)


def shifted(array, axis, step):
    size = lax.axis_size(axis)
    return lax.ppermute(array, axis, [(i, (i + step) % size) for i in range(size)])


def part(array, index, count, dim):
    size = array.shape[dim] // count
    return lax.dynamic_slice_in_dim(array, (index & (count - 1)) * size, size, dim, allow_negative_indices=False)


def made(pieces):
    return pieces(0), [pieces(step).astype(jnp.bfloat16) for step in others]


def summed(pieces, axis):
    total, sent = pieces
    received = [shifted(piece, axis, step) for piece, step in zip(sent, others)]
    for piece in received:
        total = total + piece.astype(jnp.float32)
    return total


def spread_over(array, axis):
    return [array] + [shifted(array, axis, step) for step in others]


def in_place(pieces, axis, dim):
    place = lax.axis_index(axis)
    size = pieces[0].shape[dim]
    shape = list(pieces[0].shape)
    shape[dim] = 4 * size
    whole = jnp.zeros(shape, pieces[0].dtype)
    for step, piece in zip((0, *others), pieces):
        whole = lax.dynamic_update_slice_in_dim(whole, piece, ((place - step) & 3) * size, dim, allow_negative_indices=False)
    return whole


def from_ring(whole, axis, dim):
    half = whole.shape[dim] // 2
    up, down = shifted(whole, axis, 1), shifted(whole, axis, -1)
    far = (
        shifted(lax.slice_in_dim(up, 0, half, axis=dim), axis, 1),
        shifted(lax.slice_in_dim(down, half, 2 * half, axis=dim), axis, -1),
    )
    return up, down, far


def matmul_rows(left, right):
    return lax.dot_general(left, right, (((0,), (0,)), ((), ())), preferred_element_type=jnp.float32)


def rows_for_features(hidden_a, hidden_b):
    place, count = lax.axis_index("crop"), lax.axis_size("crop")
    both = jnp.stack([hidden_a, hidden_b])
    return [part(both, place, count, 2)] + [
        shifted(part(both, place + step, count, 2), "crop", step) for step in others
    ]


def body(hidden_a, hidden_b, weight):
    view, chip, plane = lax.axis_index("core"), lax.axis_index("x"), lax.axis_index("tensor")
    total_rows = hidden_a.shape[0] * lax.axis_size("crop")
    first = view == 0
    own_rows = jnp.where(first, hidden_a, hidden_b)
    other_rows = jnp.where(first, hidden_b, hidden_a)
    own_rows, other_rows = lax.optimization_barrier((own_rows, other_rows))
    passed = jnp.dot(other_rows, weight, preferred_element_type=jnp.float32).astype(jnp.bfloat16)
    own_part = jnp.dot(own_rows, weight, preferred_element_type=jnp.float32)
    passed, own_part = shifted(passed, "core", 1), lax.optimization_barrier(own_part)
    mine_low, everyone = [], []
    pieces = []
    for chunk in range(2):
        at = lambda step: 2 * ((chip + step) & 3) + chunk
        pieces.append(
            made(
                lambda step: part(own_part, at(step), 8, 1)
                + part(passed, at(step), 8, 1).astype(jnp.float32)
            )
        )
    pieces = lax.optimization_barrier(pieces)
    for chunk in range(2):
        total = summed(pieces[chunk], "x")
        mine_low.append(total.astype(jnp.bfloat16))
    for chunk in range(2):
        everyone.append(jnp.concatenate(spread_over(mine_low[chunk], "crop")))
    mine_low = jnp.concatenate(mine_low, axis=1)
    mine = mine_low.astype(jnp.float32)
    theirs = shifted(mine_low, "core", 1).astype(jnp.float32)

    gram, rounded_all, col_means, spread = 0.0, [], [], []
    rows = mine.shape[0]
    for chunk in everyone:
        chunk = chunk.astype(jnp.float32)
        col_means.append(jnp.mean(chunk, axis=0))
        centered = chunk - col_means[-1]
        spread.append(jnp.sum(centered * centered, axis=0))
        low = centered.astype(jnp.bfloat16)
        rounded_all.append(low)
        gram = gram + jnp.einsum("rf,bf->rb", low[:rows], low, preferred_element_type=jnp.float32)
    col_means, spread = jnp.concatenate(col_means), jnp.concatenate(spread)
    rounded_all = jnp.concatenate(rounded_all, axis=1)
    deviation = jnp.sqrt(spread / (total_rows - 1.0) + epsilon)
    centered = mine - col_means

    gram, hidden_a, hidden_b = lax.optimization_barrier((gram, hidden_a, hidden_b))
    features = rows_for_features(hidden_a, hidden_b)
    half = rows // 2
    ways = (("x", chip, "tensor", gram[:half]), ("tensor", plane, "x", gram[half:]))
    sums = [
        summed(made(lambda step: part(g, at + step, 4, 0)), axis)
        for axis, at, _, g in ways
    ]
    sums = [summed(made(lambda step: s), then).astype(jnp.bfloat16) for s, (_, _, then, _) in zip(sums, ways)]
    gram_low = jnp.concatenate(
        [in_place(spread_over(s, axis), axis, 0) for s, (axis, _, _, _) in zip(sums, ways)]
    )
    gram_low, features = lax.optimization_barrier((gram_low, features))
    products = jnp.dot(gram_low, rounded_all, preferred_element_type=jnp.float32)

    hinge_rate = jnp.where(deviation < 1.0, 25.0 / ((total_rows - 1.0) * deviation), 0.0)
    cov_scale = 4.0 / (total_rows - 1.0) ** 2
    row_grads = (
        (mine - theirs) * (50.0 / total_rows)
        - hinge_rate * centered
        + cov_scale * (products - centered * spread)
    ).astype(jnp.bfloat16)

    features = jnp.stack(features, axis=1)
    own_view = jnp.where(first, features[0], features[1])
    other_view = jnp.where(first, features[1], features[0])
    wanted = (shifted(other_view, "core", 1), own_view)

    tall = jnp.concatenate(spread_over(row_grads[:half], "crop"))
    wide = in_place(spread_over(row_grads[half:], "x"), "x", 1)
    tall_up, tall_down, tall_far = from_ring(tall, "x", 0)
    wide_up, wide_down, wide_far = from_ring(wide, "crop", 0)
    parts = []
    for rows_wanted in wanted:
        near, far = rows_wanted[:, :half], rows_wanted[:, half:]
        near = near.reshape(-1, near.shape[-1])
        block = lambda array: matmul_rows(near, array)
        out = matmul_rows(far[0], wide) + matmul_rows(far[1], wide_up)
        out = out + matmul_rows(far[2], wide_down)
        talls = (tall, tall_up, tall_down, jnp.concatenate(tall_far))
        out = out + in_place([block(array) for array in talls], "x", 1)
        parts.append(out + matmul_rows(far[3], jnp.concatenate(wide_far)))
    return shifted(parts[0], "core", 1) + parts[1]


def solution(mesh):
    cores = 2
    split = Mesh(
        mesh.devices.reshape(mesh.shape["dp"] // cores, cores, *mesh.devices.shape[1:]),
        ("x", "core", "crop", "tensor"),
    )
    chips = ("x", "core")
    placed = (P("crop", chips), P("crop", chips), P(chips, "tensor"))
    return jax.shard_map(
        body,
        mesh=split,
        in_specs=placed,
        out_specs=P(("x", "core", "crop"), "tensor"),
        check_vma=False,
    )
```

profile of v0, /device:TPU:1, one launch (start us, length us, event | category | flops | bytes accessed | tf_op | source)
XLA Modules:
  0.0 223.0 jit_solution(11142869342451066217)
XLA Ops:
  0.0 1.8 broadcast_select_fusion
  1.8 1.0 copy-done.2
  2.8 3.7 %convolution_convert_fusion = bf16[512,2048]{1,0:T(8,128)(2,1)} fusion(bf16[512,1024]{1,0:T(8,128)(2,1)S(1)} %get-tuple-element.24, bf16[1024,2048]{1,0:T(8,128)(2,1)S(1)} %copy-done.2), kind=kOutput, calls=%fused_computation.1 | convolution fusion | flops 2148532224 | bytes 7340032 | tf_op jit(solution)/shard_map/dot_general | solution.py:77
  6.5 1.4 collective-permute-start
  7.9 6.5 %fusion.48 = f32[512,2048]{1,0:T(8,128)} fusion(bf16[512,1024]{1,0:T(8,128)(2,1)S(1)} %get-tuple-element.23, bf16[1024,2048]{1,0:T(8,128)(2,1)} %param.5), kind=kOutput, calls=%fused_computation.128 | convolution fusion | flops 2147483648 | bytes 9437184 | tf_op jit(solution)/shard_map/dot_general | solution.py:78
  14.4 3.8 %add_convert_fusion.4 = (bf16[512,256]{1,0:T(8,128)(2,1)}, bf16[512,256]{1,0:T(8,128)(2,1)}, bf16[512,256]{1,0:T(8,128)(2,1)}, f32[512,256]{1,0:T(8,128)S(1)}, b...) fusion(f32[512,2048]{1,0:T(8,128)} %fusion.48, ...), kind=kLoop, calls=%fused_computation.76 | loop fusion | flops 2883584 | bytes 8912928 | tf_op jit(solution)/shard_map/convert_element_type | solution.py:22
  18.2 1.3 collective-permute-start.7
  19.5 1.3 collective-permute-start.8
  20.9 1.6 collective-permute-start.9
  22.9 2.4 %collective-permute-start.2 = (bf16[512,256]{1,0:T(8,128)(2,1)}, bf16[512,256]{1,0:T(8,128)(2,1)S(1)}, u32[]{:S(2)}, u32[]{:S(2)}) collective-permute-start(bf16[512,256]{1,0:T(8,128)(2,1)} %get-tuple-element.27), channel_id=1, source_target_pairs={{0,96},{32,0},{64,32},{96,64},{1,97},{33,1},{65,33},{97,65},{2,98}... | collective-permute-start | bytes 786440 | tf_op jit(solution)/shard_map/ppermute | solution.py:13
  25.2 2.3 %collective-permute-done.7 = bf16[512,256]{1,0:T(8,128)(2,1)S(1)} collective-permute-done((bf16[512,256]{1,0:T(8,128)(2,1)}, bf16[512,256]{1,0:T(8,128)(2,1)S(1)}, u32[]{:S(2)}, u32[]{:S(2)}) %collective-permute-start.7) | collective-permute-done | bytes 262176 | tf_op jit(solution)/shard_map/ppermute | solution.py:13
  27.5 1.7 collective-permute-start.3
  29.2 5.1 %collective-permute-done.9 = bf16[512,256]{1,0:T(8,128)(2,1)S(1)} collective-permute-done((bf16[512,256]{1,0:T(8,128)(2,1)}, bf16[512,256]{1,0:T(8,128)(2,1)S(1)}, u32[]{:S(2)}, u32[]{:S(2)}) %collective-permute-start.9) | collective-permute-done | bytes 262176 | tf_op jit(solution)/shard_map/ppermute | solution.py:13
  34.4 1.4 collective-permute-start.10
  35.7 1.5 collective-permute-start.11
  37.3 1.5 collective-permute-done.1
  38.7 3.0 %collective-permute-start.12 = (bf16[512,256]{1,0:T(8,128)(2,1)S(1)}, bf16[512,256]{1,0:T(8,128)(2,1)S(1)}, u32[]{:S(2)}, u32[]{:S(2)}) collective-permute-start(bf16[512,256]{1,0:T(8,128)(2,1)S(1)} %add_convert_fusion.2), channel_id=1, source_target_pairs={{0,8},{4,12},{8,0},{12,4},{1,9},{5,13},{9,1},{13,5},{2,10},{6,14},... | collective-permute-start | bytes 786440 | tf_op jit(solution)/shard_map/ppermute | solution.py:13
  41.8 3.7 %collective-permute-done.3 = bf16[512,256]{1,0:T(8,128)(2,1)S(1)} collective-permute-done((bf16[512,256]{1,0:T(8,128)(2,1)S(1)}, bf16[512,256]{1,0:T(8,128)(2,1)S(1)}, u32[]{:S(2)}, u32[]{:S(2)}) %collective-permute-start.3) | collective-permute-done | bytes 262176 | tf_op jit(solution)/shard_map/ppermute | solution.py:13
  45.6 1.4 collective-permute-start.4
  47.0 1.5 collective-permute-start.5
  48.6 1.6 collective-permute-start.6
  50.2 1.7 collective-permute-start.35
  52.2 5.4 %collective-permute-done.4 = bf16[512,256]{1,0:T(8,128)(2,1)S(1)} collective-permute-done((bf16[512,256]{1,0:T(8,128)(2,1)S(1)}, bf16[512,256]{1,0:T(8,128)(2,1)S(1)}, u32[]{:S(2)}, u32[]{:S(2)}) %collective-permute-start.4) | collective-permute-done | bytes 262176 | tf_op jit(solution)/shard_map/ppermute | solution.py:13
  57.6 3.2 %collective-permute-done.6 = bf16[512,256]{1,0:T(8,128)(2,1)S(1)} collective-permute-done((bf16[512,256]{1,0:T(8,128)(2,1)S(1)}, bf16[512,256]{1,0:T(8,128)(2,1)S(1)}, u32[]{:S(2)}, u32[]{:S(2)}) %collective-permute-start.6) | collective-permute-done | bytes 262176 | tf_op jit(solution)/shard_map/ppermute | solution.py:13
  62.6 0.8 convolution_add_fusion
  64.2 2.4 %collective-permute-start.14 = (bf16[64,2048]{1,0:T(8,128)(2,1)S(1)}, bf16[64,2048]{1,0:T(8,128)(2,1)S(1)}, u32[]{:S(2)}, u32[]{:S(2)}) collective-permute-start(bf16[64,2048]{1,0:T(8,128)(2,1)S(1)} %get-tuple-element.63), channel_id=1, source_target_pairs={{0,96},{32,0},{64,32},{96,64},{1,97},{33,1},{65,33},{97,65},{2,98}... | collective-permute-start | bytes 786440 | tf_op jit(solution)/shard_map/ppermute | solution.py:13
  67.7 4.0 %collective-permute-done.13 = bf16[64,2048]{1,0:T(8,128)(2,1)S(1)} collective-permute-done((bf16[64,2048]{1,0:T(8,128)(2,1)S(1)}, bf16[64,2048]{1,0:T(8,128)(2,1)S(1)}, u32[]{:S(2)}, u32[]{:S(2)}) %collective-permute-start.13) | collective-permute-done | bytes 262176 | tf_op jit(solution)/shard_map/ppermute | solution.py:13
  71.7 1.7 collective-permute-start.22
  73.4 2.3 %collective-permute-start.23 = (bf16[64,2048]{1,0:T(8,128)(2,1)S(1)}, bf16[64,2048]{1,0:T(8,128)(2,1)S(1)}, u32[]{:S(2)}, u32[]{:S(2)}) collective-permute-start(bf16[64,2048]{1,0:T(8,128)(2,1)S(1)} %get-tuple-element.66), channel_id=1, source_target_pairs={{0,3},{1,0},{2,1},{3,2},{4,7},{5,4},{6,5},{7,6},{8,11},{9,8},{10,9... | collective-permute-start | bytes 786440 | tf_op jit(solution)/shard_map/ppermute | solution.py:13
  76.4 3.6 %collective-permute-start.24 = (bf16[64,2048]{1,0:T(8,128)(2,1)S(1)}, bf16[64,2048]{1,0:T(8,128)(2,1)S(1)}, u32[]{:S(2)}, u32[]{:S(2)}) collective-permute-start(bf16[64,2048]{1,0:T(8,128)(2,1)S(1)} %get-tuple-element.65), channel_id=1, source_target_pairs={{0,2},{1,3},{2,0},{3,1},{4,6},{5,7},{6,4},{7,5},{8,10},{9,11},{10,... | collective-permute-start | bytes 786440 | tf_op jit(solution)/shard_map/ppermute | solution.py:13
  80.2 0.8 collective-permute-start.16
  81.0 2.0 collective-permute-start.17
  83.0 1.8 collective-permute-done.24
  84.8 3.4 %collective-permute-start.18 = (bf16[64,2048]{1,0:T(8,128)(2,1)S(1)}, bf16[64,2048]{1,0:T(8,128)(2,1)S(1)}, u32[]{:S(2)}, u32[]{:S(2)}) collective-permute-start(bf16[64,2048]{1,0:T(8,128)(2,1)S(1)} %fusion.43), channel_id=1, source_target_pairs={{0,2},{1,3},{2,0},{3,1},{4,6},{5,7},{6,4},{7,5},{8,10},{9,11},{10,... | collective-permute-start | bytes 786440 | tf_op jit(solution)/shard_map/ppermute | solution.py:13
  88.3 2.1 collective-permute-done.16
  90.4 1.2 collective-permute-start.25
  91.6 6.5 %collective-permute-start.26 = (bf16[64,2048]{1,0:T(8,128)(2,1)S(1)}, bf16[64,2048]{1,0:T(8,128)(2,1)S(1)}, u32[]{:S(2)}, u32[]{:S(2)}) collective-permute-start(bf16[64,2048]{1,0:T(8,128)(2,1)S(1)} %fusion.44), channel_id=1, source_target_pairs={{0,96},{32,0},{64,32},{96,64},{1,97},{33,1},{65,33},{97,65},{2,98}... | collective-permute-start | bytes 786440 | tf_op jit(solution)/shard_map/ppermute | solution.py:13
  98.5 1.2 collective-permute-start.32
  99.7 4.5 %collective-permute-done.26 = bf16[64,2048]{1,0:T(8,128)(2,1)S(1)} collective-permute-done((bf16[64,2048]{1,0:T(8,128)(2,1)S(1)}, bf16[64,2048]{1,0:T(8,128)(2,1)S(1)}, u32[]{:S(2)}, u32[]{:S(2)}) %collective-permute-start.26) | collective-permute-done | bytes 262176 | tf_op jit(solution)/shard_map/ppermute | solution.py:13
  104.9 2.4 %collective-permute-start.20 = (bf16[64,2048]{1,0:T(8,128)(2,1)S(1)}, bf16[64,2048]{1,0:T(8,128)(2,1)S(1)}, u32[]{:S(2)}, u32[]{:S(2)}) collective-permute-start(bf16[64,2048]{1,0:T(8,128)(2,1)S(1)} %get-tuple-element.42), channel_id=1, source_target_pairs={{0,96},{32,0},{64,32},{96,64},{1,97},{33,1},{65,33},{97,65},{2,98}... | collective-permute-start | bytes 786440 | tf_op jit(solution)/shard_map/ppermute | solution.py:13
  107.7 5.8 %collective-permute-done.19 = bf16[64,2048]{1,0:T(8,128)(2,1)S(1)} collective-permute-done((bf16[64,2048]{1,0:T(8,128)(2,1)S(1)}, bf16[64,2048]{1,0:T(8,128)(2,1)S(1)}, u32[]{:S(2)}, u32[]{:S(2)}) %collective-permute-start.19) | collective-permute-done | bytes 262176 | tf_op jit(solution)/shard_map/ppermute | solution.py:13
  113.9 3.7 %collective-permute-start.29 = (bf16[64,2048]{1,0:T(8,128)(2,1)S(1)}, bf16[64,2048]{1,0:T(8,128)(2,1)S(1)}, u32[]{:S(2)}, u32[]{:S(2)}) collective-permute-start(bf16[64,2048]{1,0:T(8,128)(2,1)S(1)} %get-tuple-element.44), channel_id=1, source_target_pairs={{0,3},{1,0},{2,1},{3,2},{4,7},{5,4},{6,5},{7,6},{8,11},{9,8},{10,9... | collective-permute-start | bytes 786440 | tf_op jit(solution)/shard_map/ppermute | solution.py:13
  117.6 2.6 %collective-permute-done.28 = bf16[64,2048]{1,0:T(8,128)(2,1)S(1)} collective-permute-done((bf16[64,2048]{1,0:T(8,128)(2,1)S(1)}, bf16[64,2048]{1,0:T(8,128)(2,1)S(1)}, u32[]{:S(2)}, u32[]{:S(2)}) %collective-permute-start.28) | collective-permute-done | bytes 262176 | tf_op jit(solution)/shard_map/ppermute | solution.py:13
  120.2 1.1 collective-permute-start.21
  121.4 1.9 collective-permute-start.30
  123.3 3.7 %collective-permute-done.21 = bf16[64,2048]{1,0:T(8,128)(2,1)S(1)} collective-permute-done((bf16[64,2048]{1,0:T(8,128)(2,1)S(1)}, bf16[64,2048]{1,0:T(8,128)(2,1)S(1)}, u32[]{:S(2)}, u32[]{:S(2)}) %collective-permute-start.21) | collective-permute-done | bytes 262176 | tf_op jit(solution)/shard_map/ppermute | solution.py:13
  126.9 3.1 %collective-permute-start.33 = (bf16[2,512,256]{2,1,0:T(8,128)(2,1)S(1)}, bf16[2,512,256]{2,1,0:T(8,128)(2,1)S(1)}, u32[]{:S(2)}, u32[]{:S(2)}) collective-permute-start(bf16[2,512,256]{2,1,0:T(8,128)(2,1)S(1)} %get-tuple-element.57), channel_id=1, source_target_pairs={{0,8},{4,12},{8,0},{12,4},{1,9},{5,13},{9,1},{13,5},{2,10},{6,14},... | collective-permute-start | bytes 1572872 | tf_op jit(solution)/shard_map/ppermute | solution.py:13
  130.4 6.5 %collective-permute-done.33 = bf16[2,512,256]{2,1,0:T(8,128)(2,1)S(1)} collective-permute-done((bf16[2,512,256]{2,1,0:T(8,128)(2,1)S(1)}, bf16[2,512,256]{2,1,0:T(8,128)(2,1)S(1)}, u32[]{:S(2)}, u32[]{:S(2)}) %collective-permute-start.33) | collective-permute-done | bytes 524320 | tf_op jit(solution)/shard_map/ppermute | solution.py:13
  136.9 1.4 fusion.26
  138.7 2.7 %collective-permute-start.37 = (bf16[256,512]{1,0:T(8,128)(2,1)S(1)}, bf16[256,512]{1,0:T(8,128)(2,1)S(1)}, u32[]{:S(2)}, u32[]{:S(2)}) collective-permute-start(bf16[256,512]{1,0:T(8,128)(2,1)S(1)} %get-tuple-element.75), channel_id=1, source_target_pairs={{0,96},{32,0},{64,32},{96,64},{1,97},{33,1},{65,33},{97,65},{2,98}... | collective-permute-start | bytes 786440 | tf_op jit(solution)/shard_map/ppermute | solution.py:13
  141.3 1.1 collective-permute-start.41
  142.5 1.5 collective-permute-start.42
  144.0 1.8 collective-permute-start.43
  146.2 4.9 %collective-permute-done.41 = bf16[256,512]{1,0:T(8,128)(2,1)S(1)} collective-permute-done((bf16[256,512]{1,0:T(8,128)(2,1)S(1)}, bf16[256,512]{1,0:T(8,128)(2,1)S(1)}, u32[]{:S(2)}, u32[]{:S(2)}) %collective-permute-start.41) | collective-permute-done | bytes 262176 | tf_op jit(solution)/shard_map/ppermute | solution.py:13
  151.4 18.4 %collective-permute-start.34 = (bf16[4,512,256]{2,1,0:T(8,128)(2,1)S(1)}, bf16[4,512,256]{2,1,0:T(8,128)(2,1)S(1)}, u32[]{:S(2)}, u32[]{:S(2)}) collective-permute-start(bf16[4,512,256]{2,1,0:T(8,128)(2,1)S(1)} %get-tuple-element.56), channel_id=1, source_target_pairs={{0,16},{16,0},{1,17},{17,1},{2,18},{18,2},{3,19},{19,3},{4,20},{20... | collective-permute-start | bytes 3145736 | tf_op jit(solution)/shard_map/ppermute | solution.py:13
  169.9 2.7 %collective-permute-start.45 = (bf16[1024,512]{1,0:T(8,128)(2,1)S(1)}, bf16[1024,512]{1,0:T(8,128)(2,1)S(1)}, u32[]{:S(2)}, u32[]{:S(2)}) collective-permute-start(bf16[1024,512]{1,0:T(8,128)(2,1)S(1)} %pad_maximum_fusion.4), channel_id=1, source_target_pairs={{0,96},{32,0},{64,32},{96,64},{1,97},{33,1},{65,33},{97,65},{2,98}... | collective-permute-start | bytes 3145736 | tf_op jit(solution)/shard_map/ppermute | solution.py:13
  173.1 2.3 %collective-permute-start.40 = (bf16[256,2048]{1,0:T(8,128)(2,1)S(1)}, bf16[256,2048]{1,0:T(8,128)(2,1)S(1)}, u32[]{:S(2)}, u32[]{:S(2)}) collective-permute-start(bf16[256,2048]{1,0:T(8,128)(2,1)S(1)} %constant_dynamic-update-slice_fusion), channel_id=1, source_target_pairs={{0,12},{4,0},{8,4},{12,8},{1,13},{5,1},{9,5},{13,9},{2,14},{6,2},{... | collective-permute-start | bytes 3145736 | tf_op jit(solution)/shard_map/ppermute | solution.py:13
  176.9 20.1 %collective-permute-done.44 = bf16[1024,512]{1,0:T(8,128)(2,1)S(1)} collective-permute-done((bf16[1024,512]{1,0:T(8,128)(2,1)S(1)}, bf16[1024,512]{1,0:T(8,128)(2,1)S(1)}, u32[]{:S(2)}, u32[]{:S(2)}) %collective-permute-start.44) | collective-permute-done | bytes 1048608 | tf_op jit(solution)/shard_map/ppermute | solution.py:13
  197.2 2.7 %collective-permute-start.47 = (bf16[512,512]{1,0:T(8,128)(2,1)S(1)}, bf16[512,512]{1,0:T(8,128)(2,1)S(1)}, u32[]{:S(2)}, u32[]{:S(2)}) collective-permute-start(bf16[512,512]{1,0:T(8,128)(2,1)S(1)} %slice.111), channel_id=1, source_target_pairs={{0,96},{32,0},{64,32},{96,64},{1,97},{33,1},{65,33},{97,65},{2,98}... | collective-permute-start | bytes 1572872 | tf_op jit(solution)/shard_map/ppermute | solution.py:13
  200.1 2.7 %collective-permute-start.49 = (bf16[128,2048]{1,0:T(8,128)(2,1)S(1)}, bf16[128,2048]{1,0:T(8,128)(2,1)S(1)}, u32[]{:S(2)}, u32[]{:S(2)}) collective-permute-start(bf16[128,2048]{1,0:T(8,128)(2,1)S(1)} %slice.114), channel_id=1, source_target_pairs={{0,12},{4,0},{8,4},{12,8},{1,13},{5,1},{9,5},{13,9},{2,14},{6,2},{... | collective-permute-start | bytes 1572872 | tf_op jit(solution)/shard_map/ppermute | solution.py:13
  204.7 4.8 %collective-permute-done.46 = bf16[512,512]{1,0:T(8,128)(2,1)S(1)} collective-permute-done((bf16[512,512]{1,0:T(8,128)(2,1)S(1)}, bf16[512,512]{1,0:T(8,128)(2,1)S(1)}, u32[]{:S(2)}, u32[]{:S(2)}) %collective-permute-start.46) | collective-permute-done | bytes 524320 | tf_op jit(solution)/shard_map/ppermute | solution.py:13
  209.6 2.2 %collective-permute-done.48 = bf16[128,2048]{1,0:T(8,128)(2,1)S(1)} collective-permute-done((bf16[128,2048]{1,0:T(8,128)(2,1)S(1)}, bf16[128,2048]{1,0:T(8,128)(2,1)S(1)}, u32[]{:S(2)}, u32[]{:S(2)}) %collective-permute-start.48) | collective-permute-done | bytes 524320 | tf_op jit(solution)/shard_map/ppermute | solution.py:13
  213.5 4.1 %collective-permute-start.50 = (f32[256,2048]{1,0:T(8,128)S(1)}, f32[256,2048]{1,0:T(8,128)S(1)}, u32[]{:S(2)}, u32[]{:S(2)}) collective-permute-start(f32[256,2048]{1,0:T(8,128)S(1)} %fusion.5), channel_id=1, source_target_pairs={{0,16},{16,0},{1,17},{17,1},{2,18},{18,2},{3,19},{19,3},{4,20},{20... | collective-permute-start | bytes 6291464 | tf_op jit(solution)/shard_map/ppermute | solution.py:13
  221.4 1.6 add.233
  (116 shorter events, 18.5 us)
Async XLA Ops:
  0.0 2.8 %copy-start.2 = (bf16[1024,2048]{1,0:T(8,128)(2,1)S(1)}, bf16[1024,2048]{1,0:T(8,128)(2,1)}, u32[]{:S(2)}) copy-start(bf16[1024,2048]{1,0:T(8,128)(2,1)} %param.5) | copy-start | bytes 12582916
  6.5 7.9 %collective-permute-start = (bf16[512,2048]{1,0:T(8,128)(2,1)}, bf16[512,2048]{1,0:T(8,128)(2,1)S(1)}, u32[]{:S(2)}, u32[]{:S(2)}) collective-permute-start(bf16[512,2048]{1,0:T(8,128)(2,1)} %convolution_convert_fusion), channel_id=1, source_target_pairs={{0,16},{16,0},{1,17},{17,1},{2,18},{18,2},{3,19},{19,3},{4,20},{20... | collective-permute-start | bytes 6291464 | tf_op jit(solution)/shard_map/ppermute | solution.py:13
  18.2 9.3 %collective-permute-start.7 = (bf16[512,256]{1,0:T(8,128)(2,1)}, bf16[512,256]{1,0:T(8,128)(2,1)S(1)}, u32[]{:S(2)}, u32[]{:S(2)}) collective-permute-start(bf16[512,256]{1,0:T(8,128)(2,1)} %get-tuple-element.30), channel_id=1, source_target_pairs={{0,32},{32,64},{64,96},{96,0},{1,33},{33,65},{65,97},{97,1},{2,34}... | collective-permute-start | bytes 786440 | tf_op jit(solution)/shard_map/ppermute | solution.py:13
  19.5 9.6 %collective-permute-start.8 = (bf16[512,256]{1,0:T(8,128)(2,1)}, bf16[512,256]{1,0:T(8,128)(2,1)S(1)}, u32[]{:S(2)}, u32[]{:S(2)}) collective-permute-start(bf16[512,256]{1,0:T(8,128)(2,1)} %get-tuple-element.31), channel_id=1, source_target_pairs={{0,96},{32,0},{64,32},{96,64},{1,97},{33,1},{65,33},{97,65},{2,98}... | collective-permute-start | bytes 786440 | tf_op jit(solution)/shard_map/ppermute | solution.py:13
  20.9 13.4 %collective-permute-start.9 = (bf16[512,256]{1,0:T(8,128)(2,1)}, bf16[512,256]{1,0:T(8,128)(2,1)S(1)}, u32[]{:S(2)}, u32[]{:S(2)}) collective-permute-start(bf16[512,256]{1,0:T(8,128)(2,1)} %get-tuple-element.32), channel_id=1, source_target_pairs={{0,64},{32,96},{64,0},{96,32},{1,65},{33,97},{65,1},{97,33},{2,66}... | collective-permute-start | bytes 786440 | tf_op jit(solution)/shard_map/ppermute | solution.py:13
  22.5 16.2 %collective-permute-start.1 = (bf16[512,256]{1,0:T(8,128)(2,1)}, bf16[512,256]{1,0:T(8,128)(2,1)S(1)}, u32[]{:S(2)}, u32[]{:S(2)}) collective-permute-start(bf16[512,256]{1,0:T(8,128)(2,1)} %get-tuple-element.26), channel_id=1, source_target_pairs={{0,32},{32,64},{64,96},{96,0},{1,33},{33,65},{65,97},{97,1},{2,34}... | collective-permute-start | bytes 786440 | tf_op jit(solution)/shard_map/ppermute | solution.py:13
  22.9 18.9 %collective-permute-start.2 = (bf16[512,256]{1,0:T(8,128)(2,1)}, bf16[512,256]{1,0:T(8,128)(2,1)S(1)}, u32[]{:S(2)}, u32[]{:S(2)}) collective-permute-start(bf16[512,256]{1,0:T(8,128)(2,1)} %get-tuple-element.27), channel_id=1, source_target_pairs={{0,96},{32,0},{64,32},{96,64},{1,97},{33,1},{65,33},{97,65},{2,98}... | collective-permute-start | bytes 786440 | tf_op jit(solution)/shard_map/ppermute | solution.py:13
  27.5 18.0 %collective-permute-start.3 = (bf16[512,256]{1,0:T(8,128)(2,1)S(1)}, bf16[512,256]{1,0:T(8,128)(2,1)S(1)}, u32[]{:S(2)}, u32[]{:S(2)}) collective-permute-start(bf16[512,256]{1,0:T(8,128)(2,1)S(1)} %get-tuple-element.28), channel_id=1, source_target_pairs={{0,64},{32,96},{64,0},{96,32},{1,65},{33,97},{65,1},{97,33},{2,66}... | collective-permute-start | bytes 786440 | tf_op jit(solution)/shard_map/ppermute | solution.py:13
  34.4 14.2 %collective-permute-start.10 = (bf16[512,256]{1,0:T(8,128)(2,1)S(1)}, bf16[512,256]{1,0:T(8,128)(2,1)S(1)}, u32[]{:S(2)}, u32[]{:S(2)}) collective-permute-start(bf16[512,256]{1,0:T(8,128)(2,1)S(1)} %add_convert_fusion.2), channel_id=1, source_target_pairs={{0,4},{4,8},{8,12},{12,0},{1,5},{5,9},{9,13},{13,1},{2,6},{6,10},{... | collective-permute-start | bytes 786440 | tf_op jit(solution)/shard_map/ppermute | solution.py:13
  35.7 14.5 %collective-permute-start.11 = (bf16[512,256]{1,0:T(8,128)(2,1)S(1)}, bf16[512,256]{1,0:T(8,128)(2,1)S(1)}, u32[]{:S(2)}, u32[]{:S(2)}) collective-permute-start(bf16[512,256]{1,0:T(8,128)(2,1)S(1)} %add_convert_fusion.2), channel_id=1, source_target_pairs={{0,12},{4,0},{8,4},{12,8},{1,13},{5,1},{9,5},{13,9},{2,14},{6,2},{... | collective-permute-start | bytes 786440 | tf_op jit(solution)/shard_map/ppermute | solution.py:13
  38.7 13.2 %collective-permute-start.12 = (bf16[512,256]{1,0:T(8,128)(2,1)S(1)}, bf16[512,256]{1,0:T(8,128)(2,1)S(1)}, u32[]{:S(2)}, u32[]{:S(2)}) collective-permute-start(bf16[512,256]{1,0:T(8,128)(2,1)S(1)} %add_convert_fusion.2), channel_id=1, source_target_pairs={{0,8},{4,12},{8,0},{12,4},{1,9},{5,13},{9,1},{13,5},{2,10},{6,14},... | collective-permute-start | bytes 786440 | tf_op jit(solution)/shard_map/ppermute | solution.py:13
  45.6 12.0 %collective-permute-start.4 = (bf16[512,256]{1,0:T(8,128)(2,1)S(1)}, bf16[512,256]{1,0:T(8,128)(2,1)S(1)}, u32[]{:S(2)}, u32[]{:S(2)}) collective-permute-start(bf16[512,256]{1,0:T(8,128)(2,1)S(1)} %add_convert_fusion.3), channel_id=1, source_target_pairs={{0,4},{4,8},{8,12},{12,0},{1,5},{5,9},{9,13},{13,1},{2,6},{6,10},{... | collective-permute-start | bytes 786440 | tf_op jit(solution)/shard_map/ppermute | solution.py:13
  47.0 10.6 %collective-permute-start.5 = (bf16[512,256]{1,0:T(8,128)(2,1)S(1)}, bf16[512,256]{1,0:T(8,128)(2,1)S(1)}, u32[]{:S(2)}, u32[]{:S(2)}) collective-permute-start(bf16[512,256]{1,0:T(8,128)(2,1)S(1)} %add_convert_fusion.3), channel_id=1, source_target_pairs={{0,12},{4,0},{8,4},{12,8},{1,13},{5,1},{9,5},{13,9},{2,14},{6,2},{... | collective-permute-start | bytes 786440 | tf_op jit(solution)/shard_map/ppermute | solution.py:13
  48.6 12.2 %collective-permute-start.6 = (bf16[512,256]{1,0:T(8,128)(2,1)S(1)}, bf16[512,256]{1,0:T(8,128)(2,1)S(1)}, u32[]{:S(2)}, u32[]{:S(2)}) collective-permute-start(bf16[512,256]{1,0:T(8,128)(2,1)S(1)} %add_convert_fusion.3), channel_id=1, source_target_pairs={{0,8},{4,12},{8,0},{12,4},{1,9},{5,13},{9,1},{13,5},{2,10},{6,14},... | collective-permute-start | bytes 786440 | tf_op jit(solution)/shard_map/ppermute | solution.py:13
  50.2 86.7 %collective-permute-start.35 = (bf16[512,512]{1,0:T(8,128)(2,1)S(1)}, bf16[512,512]{1,0:T(8,128)(2,1)S(1)}, u32[]{:S(2)}, u32[]{:S(2)}) collective-permute-start(bf16[512,512]{1,0:T(8,128)(2,1)S(1)} %pad_maximum_fusion.5), channel_id=1, source_target_pairs={{0,16},{16,0},{1,17},{17,1},{2,18},{18,2},{3,19},{19,3},{4,20},{20... | collective-permute-start | bytes 1572872 | tf_op jit(solution)/shard_map/ppermute | solution.py:13
  63.4 3.2 %copy-start.1 = (bf16[512,1024]{1,0:T(8,128)(2,1)S(1)}, bf16[512,1024]{1,0:T(8,128)(2,1)}, u32[]{:S(2)}) copy-start(bf16[512,1024]{1,0:T(8,128)(2,1)} %param.3) | copy-start | bytes 3145732
  63.7 2.9 %copy-start = (bf16[512,1024]{1,0:T(8,128)(2,1)S(1)}, bf16[512,1024]{1,0:T(8,128)(2,1)}, u32[]{:S(2)}) copy-start(bf16[512,1024]{1,0:T(8,128)(2,1)} %param.4) | copy-start | bytes 3145732
  63.8 7.9 %collective-permute-start.13 = (bf16[64,2048]{1,0:T(8,128)(2,1)S(1)}, bf16[64,2048]{1,0:T(8,128)(2,1)S(1)}, u32[]{:S(2)}, u32[]{:S(2)}) collective-permute-start(bf16[64,2048]{1,0:T(8,128)(2,1)S(1)} %get-tuple-element.61), channel_id=1, source_target_pairs={{0,32},{32,64},{64,96},{96,0},{1,33},{33,65},{65,97},{97,1},{2,34}... | collective-permute-start | bytes 786440 | tf_op jit(solution)/shard_map/ppermute | solution.py:13
  64.2 9.2 %collective-permute-start.14 = (bf16[64,2048]{1,0:T(8,128)(2,1)S(1)}, bf16[64,2048]{1,0:T(8,128)(2,1)S(1)}, u32[]{:S(2)}, u32[]{:S(2)}) collective-permute-start(bf16[64,2048]{1,0:T(8,128)(2,1)S(1)} %get-tuple-element.63), channel_id=1, source_target_pairs={{0,96},{32,0},{64,32},{96,64},{1,97},{33,1},{65,33},{97,65},{2,98}... | collective-permute-start | bytes 786440 | tf_op jit(solution)/shard_map/ppermute | solution.py:13
  66.6 9.9 %collective-permute-start.15 = (bf16[64,2048]{1,0:T(8,128)(2,1)S(1)}, bf16[64,2048]{1,0:T(8,128)(2,1)S(1)}, u32[]{:S(2)}, u32[]{:S(2)}) collective-permute-start(bf16[64,2048]{1,0:T(8,128)(2,1)S(1)} %get-tuple-element.62), channel_id=1, source_target_pairs={{0,64},{32,96},{64,0},{96,32},{1,65},{33,97},{65,1},{97,33},{2,66}... | collective-permute-start | bytes 786440 | tf_op jit(solution)/shard_map/ppermute | solution.py:13
  66.9 63.5 %collective-permute-start.31 = (bf16[2,512,256]{2,1,0:T(8,128)(2,1)S(1)}, bf16[2,512,256]{2,1,0:T(8,128)(2,1)S(1)}, u32[]{:S(2)}, u32[]{:S(2)}) collective-permute-start(bf16[2,512,256]{2,1,0:T(8,128)(2,1)S(1)} %get-tuple-element.59), channel_id=1, source_target_pairs={{0,4},{4,8},{8,12},{12,0},{1,5},{5,9},{9,13},{13,1},{2,6},{6,10},{... | collective-permute-start | bytes 1572872 | tf_op jit(solution)/shard_map/ppermute | solution.py:13
  71.7 8.5 %collective-permute-start.22 = (bf16[64,2048]{1,0:T(8,128)(2,1)S(1)}, bf16[64,2048]{1,0:T(8,128)(2,1)S(1)}, u32[]{:S(2)}, u32[]{:S(2)}) collective-permute-start(bf16[64,2048]{1,0:T(8,128)(2,1)S(1)} %get-tuple-element.64), channel_id=1, source_target_pairs={{0,1},{1,2},{2,3},{3,0},{4,5},{5,6},{6,7},{7,4},{8,9},{9,10},{10,1... | collective-permute-start | bytes 786440 | tf_op jit(solution)/shard_map/ppermute | solution.py:13
  73.4 7.6 %collective-permute-start.23 = (bf16[64,2048]{1,0:T(8,128)(2,1)S(1)}, bf16[64,2048]{1,0:T(8,128)(2,1)S(1)}, u32[]{:S(2)}, u32[]{:S(2)}) collective-permute-start(bf16[64,2048]{1,0:T(8,128)(2,1)S(1)} %get-tuple-element.66), channel_id=1, source_target_pairs={{0,3},{1,0},{2,1},{3,2},{4,7},{5,4},{6,5},{7,6},{8,11},{9,8},{10,9... | collective-permute-start | bytes 786440 | tf_op jit(solution)/shard_map/ppermute | solution.py:13
  76.4 8.3 %collective-permute-start.24 = (bf16[64,2048]{1,0:T(8,128)(2,1)S(1)}, bf16[64,2048]{1,0:T(8,128)(2,1)S(1)}, u32[]{:S(2)}, u32[]{:S(2)}) collective-permute-start(bf16[64,2048]{1,0:T(8,128)(2,1)S(1)} %get-tuple-element.65), channel_id=1, source_target_pairs={{0,2},{1,3},{2,0},{3,1},{4,6},{5,7},{6,4},{7,5},{8,10},{9,11},{10,... | collective-permute-start | bytes 786440 | tf_op jit(solution)/shard_map/ppermute | solution.py:13
  80.2 10.2 %collective-permute-start.16 = (bf16[64,2048]{1,0:T(8,128)(2,1)S(1)}, bf16[64,2048]{1,0:T(8,128)(2,1)S(1)}, u32[]{:S(2)}, u32[]{:S(2)}) collective-permute-start(bf16[64,2048]{1,0:T(8,128)(2,1)S(1)} %fusion.43), channel_id=1, source_target_pairs={{0,1},{1,2},{2,3},{3,0},{4,5},{5,6},{6,7},{7,4},{8,9},{9,10},{10,1... | collective-permute-start | bytes 786440 | tf_op jit(solution)/shard_map/ppermute | solution.py:13
  81.0 10.6 %collective-permute-start.17 = (bf16[64,2048]{1,0:T(8,128)(2,1)S(1)}, bf16[64,2048]{1,0:T(8,128)(2,1)S(1)}, u32[]{:S(2)}, u32[]{:S(2)}) collective-permute-start(bf16[64,2048]{1,0:T(8,128)(2,1)S(1)} %fusion.43), channel_id=1, source_target_pairs={{0,3},{1,0},{2,1},{3,2},{4,7},{5,4},{6,5},{7,6},{8,11},{9,8},{10,9... | collective-permute-start | bytes 786440 | tf_op jit(solution)/shard_map/ppermute | solution.py:13
  84.8 13.3 %collective-permute-start.18 = (bf16[64,2048]{1,0:T(8,128)(2,1)S(1)}, bf16[64,2048]{1,0:T(8,128)(2,1)S(1)}, u32[]{:S(2)}, u32[]{:S(2)}) collective-permute-start(bf16[64,2048]{1,0:T(8,128)(2,1)S(1)} %fusion.43), channel_id=1, source_target_pairs={{0,2},{1,3},{2,0},{3,1},{4,6},{5,7},{6,4},{7,5},{8,10},{9,11},{10,... | collective-permute-start | bytes 786440 | tf_op jit(solution)/shard_map/ppermute | solution.py:13
  90.4 8.1 %collective-permute-start.25 = (bf16[64,2048]{1,0:T(8,128)(2,1)S(1)}, bf16[64,2048]{1,0:T(8,128)(2,1)S(1)}, u32[]{:S(2)}, u32[]{:S(2)}) collective-permute-start(bf16[64,2048]{1,0:T(8,128)(2,1)S(1)} %fusion.44), channel_id=1, source_target_pairs={{0,32},{32,64},{64,96},{96,0},{1,33},{33,65},{65,97},{97,1},{2,34}... | collective-permute-start | bytes 786440 | tf_op jit(solution)/shard_map/ppermute | solution.py:13
  91.6 12.6 %collective-permute-start.26 = (bf16[64,2048]{1,0:T(8,128)(2,1)S(1)}, bf16[64,2048]{1,0:T(8,128)(2,1)S(1)}, u32[]{:S(2)}, u32[]{:S(2)}) collective-permute-start(bf16[64,2048]{1,0:T(8,128)(2,1)S(1)} %fusion.44), channel_id=1, source_target_pairs={{0,96},{32,0},{64,32},{96,64},{1,97},{33,1},{65,33},{97,65},{2,98}... | collective-permute-start | bytes 786440 | tf_op jit(solution)/shard_map/ppermute | solution.py:13
  98.1 6.8 %collective-permute-start.27 = (bf16[64,2048]{1,0:T(8,128)(2,1)S(1)}, bf16[64,2048]{1,0:T(8,128)(2,1)S(1)}, u32[]{:S(2)}, u32[]{:S(2)}) collective-permute-start(bf16[64,2048]{1,0:T(8,128)(2,1)S(1)} %fusion.44), channel_id=1, source_target_pairs={{0,64},{32,96},{64,0},{96,32},{1,65},{33,97},{65,1},{97,33},{2,66}... | collective-permute-start | bytes 786440 | tf_op jit(solution)/shard_map/ppermute | solution.py:13
  98.5 31.9 %collective-permute-start.32 = (bf16[2,512,256]{2,1,0:T(8,128)(2,1)S(1)}, bf16[2,512,256]{2,1,0:T(8,128)(2,1)S(1)}, u32[]{:S(2)}, u32[]{:S(2)}) collective-permute-start(bf16[2,512,256]{2,1,0:T(8,128)(2,1)S(1)} %get-tuple-element.60), channel_id=1, source_target_pairs={{0,12},{4,0},{8,4},{12,8},{1,13},{5,1},{9,5},{13,9},{2,14},{6,2},{... | collective-permute-start | bytes 1572872 | tf_op jit(solution)/shard_map/ppermute | solution.py:13
  104.2 9.3 %collective-permute-start.19 = (bf16[64,2048]{1,0:T(8,128)(2,1)S(1)}, bf16[64,2048]{1,0:T(8,128)(2,1)S(1)}, u32[]{:S(2)}, u32[]{:S(2)}) collective-permute-start(bf16[64,2048]{1,0:T(8,128)(2,1)S(1)} %get-tuple-element.42), channel_id=1, source_target_pairs={{0,32},{32,64},{64,96},{96,0},{1,33},{33,65},{65,97},{97,1},{2,34}... | collective-permute-start | bytes 786440 | tf_op jit(solution)/shard_map/ppermute | solution.py:13
  104.9 9.0 %collective-permute-start.20 = (bf16[64,2048]{1,0:T(8,128)(2,1)S(1)}, bf16[64,2048]{1,0:T(8,128)(2,1)S(1)}, u32[]{:S(2)}, u32[]{:S(2)}) collective-permute-start(bf16[64,2048]{1,0:T(8,128)(2,1)S(1)} %get-tuple-element.42), channel_id=1, source_target_pairs={{0,96},{32,0},{64,32},{96,64},{1,97},{33,1},{65,33},{97,65},{2,98}... | collective-permute-start | bytes 786440 | tf_op jit(solution)/shard_map/ppermute | solution.py:13
  113.5 6.7 %collective-permute-start.28 = (bf16[64,2048]{1,0:T(8,128)(2,1)S(1)}, bf16[64,2048]{1,0:T(8,128)(2,1)S(1)}, u32[]{:S(2)}, u32[]{:S(2)}) collective-permute-start(bf16[64,2048]{1,0:T(8,128)(2,1)S(1)} %get-tuple-element.44), channel_id=1, source_target_pairs={{0,1},{1,2},{2,3},{3,0},{4,5},{5,6},{6,7},{7,4},{8,9},{9,10},{10,1... | collective-permute-start | bytes 786440 | tf_op jit(solution)/shard_map/ppermute | solution.py:13
  113.9 7.4 %collective-permute-start.29 = (bf16[64,2048]{1,0:T(8,128)(2,1)S(1)}, bf16[64,2048]{1,0:T(8,128)(2,1)S(1)}, u32[]{:S(2)}, u32[]{:S(2)}) collective-permute-start(bf16[64,2048]{1,0:T(8,128)(2,1)S(1)} %get-tuple-element.44), channel_id=1, source_target_pairs={{0,3},{1,0},{2,1},{3,2},{4,7},{5,4},{6,5},{7,6},{8,11},{9,8},{10,9... | collective-permute-start | bytes 786440 | tf_op jit(solution)/shard_map/ppermute | solution.py:13
  120.2 6.7 %collective-permute-start.21 = (bf16[64,2048]{1,0:T(8,128)(2,1)S(1)}, bf16[64,2048]{1,0:T(8,128)(2,1)S(1)}, u32[]{:S(2)}, u32[]{:S(2)}) collective-permute-start(bf16[64,2048]{1,0:T(8,128)(2,1)S(1)} %get-tuple-element.42), channel_id=1, source_target_pairs={{0,64},{32,96},{64,0},{96,32},{1,65},{33,97},{65,1},{97,33},{2,66}... | collective-permute-start | bytes 786440 | tf_op jit(solution)/shard_map/ppermute | solution.py:13
  121.4 8.7 %collective-permute-start.30 = (bf16[64,2048]{1,0:T(8,128)(2,1)S(1)}, bf16[64,2048]{1,0:T(8,128)(2,1)S(1)}, u32[]{:S(2)}, u32[]{:S(2)}) collective-permute-start(bf16[64,2048]{1,0:T(8,128)(2,1)S(1)} %get-tuple-element.44), channel_id=1, source_target_pairs={{0,2},{1,3},{2,0},{3,1},{4,6},{5,7},{6,4},{7,5},{8,10},{9,11},{10,... | collective-permute-start | bytes 786440 | tf_op jit(solution)/shard_map/ppermute | solution.py:13
  126.9 10.0 %collective-permute-start.33 = (bf16[2,512,256]{2,1,0:T(8,128)(2,1)S(1)}, bf16[2,512,256]{2,1,0:T(8,128)(2,1)S(1)}, u32[]{:S(2)}, u32[]{:S(2)}) collective-permute-start(bf16[2,512,256]{2,1,0:T(8,128)(2,1)S(1)} %get-tuple-element.57), channel_id=1, source_target_pairs={{0,8},{4,12},{8,0},{12,4},{1,9},{5,13},{9,1},{13,5},{2,10},{6,14},... | collective-permute-start | bytes 1572872 | tf_op jit(solution)/shard_map/ppermute | solution.py:13
  138.6 31.3 %collective-permute-start.36 = (bf16[256,512]{1,0:T(8,128)(2,1)S(1)}, bf16[256,512]{1,0:T(8,128)(2,1)S(1)}, u32[]{:S(2)}, u32[]{:S(2)}) collective-permute-start(bf16[256,512]{1,0:T(8,128)(2,1)S(1)} %get-tuple-element.75), channel_id=1, source_target_pairs={{0,32},{32,64},{64,96},{96,0},{1,33},{33,65},{65,97},{97,1},{2,34}... | collective-permute-start | bytes 786440 | tf_op jit(solution)/shard_map/ppermute | solution.py:13
  138.7 33.9 %collective-permute-start.37 = (bf16[256,512]{1,0:T(8,128)(2,1)S(1)}, bf16[256,512]{1,0:T(8,128)(2,1)S(1)}, u32[]{:S(2)}, u32[]{:S(2)}) collective-permute-start(bf16[256,512]{1,0:T(8,128)(2,1)S(1)} %get-tuple-element.75), channel_id=1, source_target_pairs={{0,96},{32,0},{64,32},{96,64},{1,97},{33,1},{65,33},{97,65},{2,98}... | collective-permute-start | bytes 786440 | tf_op jit(solution)/shard_map/ppermute | solution.py:13
  141.3 9.7 %collective-permute-start.41 = (bf16[256,512]{1,0:T(8,128)(2,1)S(1)}, bf16[256,512]{1,0:T(8,128)(2,1)S(1)}, u32[]{:S(2)}, u32[]{:S(2)}) collective-permute-start(bf16[256,512]{1,0:T(8,128)(2,1)S(1)} %get-tuple-element.73), channel_id=1, source_target_pairs={{0,4},{4,8},{8,12},{12,0},{1,5},{5,9},{9,13},{13,1},{2,6},{6,10},{... | collective-permute-start | bytes 786440 | tf_op jit(solution)/shard_map/ppermute | solution.py:13
  142.5 8.9 %collective-permute-start.42 = (bf16[256,512]{1,0:T(8,128)(2,1)S(1)}, bf16[256,512]{1,0:T(8,128)(2,1)S(1)}, u32[]{:S(2)}, u32[]{:S(2)}) collective-permute-start(bf16[256,512]{1,0:T(8,128)(2,1)S(1)} %get-tuple-element.73), channel_id=1, source_target_pairs={{0,12},{4,0},{8,4},{12,8},{1,13},{5,1},{9,5},{13,9},{2,14},{6,2},{... | collective-permute-start | bytes 786440 | tf_op jit(solution)/shard_map/ppermute | solution.py:13
  144.0 25.7 %collective-permute-start.43 = (bf16[256,512]{1,0:T(8,128)(2,1)S(1)}, bf16[256,512]{1,0:T(8,128)(2,1)S(1)}, u32[]{:S(2)}, u32[]{:S(2)}) collective-permute-start(bf16[256,512]{1,0:T(8,128)(2,1)S(1)} %get-tuple-element.73), channel_id=1, source_target_pairs={{0,8},{4,12},{8,0},{12,4},{1,9},{5,13},{9,1},{13,5},{2,10},{6,14},... | collective-permute-start | bytes 786440 | tf_op jit(solution)/shard_map/ppermute | solution.py:13
  151.1 21.6 %collective-permute-start.38 = (bf16[256,512]{1,0:T(8,128)(2,1)S(1)}, bf16[256,512]{1,0:T(8,128)(2,1)S(1)}, u32[]{:S(2)}, u32[]{:S(2)}) collective-permute-start(bf16[256,512]{1,0:T(8,128)(2,1)S(1)} %get-tuple-element.75), channel_id=1, source_target_pairs={{0,64},{32,96},{64,0},{96,32},{1,65},{33,97},{65,1},{97,33},{2,66}... | collective-permute-start | bytes 786440 | tf_op jit(solution)/shard_map/ppermute | solution.py:13
  151.4 24.8 %collective-permute-start.34 = (bf16[4,512,256]{2,1,0:T(8,128)(2,1)S(1)}, bf16[4,512,256]{2,1,0:T(8,128)(2,1)S(1)}, u32[]{:S(2)}, u32[]{:S(2)}) collective-permute-start(bf16[4,512,256]{2,1,0:T(8,128)(2,1)S(1)} %get-tuple-element.56), channel_id=1, source_target_pairs={{0,16},{16,0},{1,17},{17,1},{2,18},{18,2},{3,19},{19,3},{4,20},{20... | collective-permute-start | bytes 3145736 | tf_op jit(solution)/shard_map/ppermute | solution.py:13
  169.8 27.2 %collective-permute-start.44 = (bf16[1024,512]{1,0:T(8,128)(2,1)S(1)}, bf16[1024,512]{1,0:T(8,128)(2,1)S(1)}, u32[]{:S(2)}, u32[]{:S(2)}) collective-permute-start(bf16[1024,512]{1,0:T(8,128)(2,1)S(1)} %pad_maximum_fusion.4), channel_id=1, source_target_pairs={{0,32},{32,64},{64,96},{96,0},{1,33},{33,65},{65,97},{97,1},{2,34}... | collective-permute-start | bytes 3145736 | tf_op jit(solution)/shard_map/ppermute | solution.py:13
  169.9 27.2 %collective-permute-start.45 = (bf16[1024,512]{1,0:T(8,128)(2,1)S(1)}, bf16[1024,512]{1,0:T(8,128)(2,1)S(1)}, u32[]{:S(2)}, u32[]{:S(2)}) collective-permute-start(bf16[1024,512]{1,0:T(8,128)(2,1)S(1)} %pad_maximum_fusion.4), channel_id=1, source_target_pairs={{0,96},{32,0},{64,32},{96,64},{1,97},{33,1},{65,33},{97,65},{2,98}... | collective-permute-start | bytes 3145736 | tf_op jit(solution)/shard_map/ppermute | solution.py:13
  172.7 27.2 %collective-permute-start.39 = (bf16[256,2048]{1,0:T(8,128)(2,1)S(1)}, bf16[256,2048]{1,0:T(8,128)(2,1)S(1)}, u32[]{:S(2)}, u32[]{:S(2)}) collective-permute-start(bf16[256,2048]{1,0:T(8,128)(2,1)S(1)} %constant_dynamic-update-slice_fusion), channel_id=1, source_target_pairs={{0,4},{4,8},{8,12},{12,0},{1,5},{5,9},{9,13},{13,1},{2,6},{6,10},{... | collective-permute-start | bytes 3145736 | tf_op jit(solution)/shard_map/ppermute | solution.py:13
  173.1 27.0 %collective-permute-start.40 = (bf16[256,2048]{1,0:T(8,128)(2,1)S(1)}, bf16[256,2048]{1,0:T(8,128)(2,1)S(1)}, u32[]{:S(2)}, u32[]{:S(2)}) collective-permute-start(bf16[256,2048]{1,0:T(8,128)(2,1)S(1)} %constant_dynamic-update-slice_fusion), channel_id=1, source_target_pairs={{0,12},{4,0},{8,4},{12,8},{1,13},{5,1},{9,5},{13,9},{2,14},{6,2},{... | collective-permute-start | bytes 3145736 | tf_op jit(solution)/shard_map/ppermute | solution.py:13
  197.1 12.4 %collective-permute-start.46 = (bf16[512,512]{1,0:T(8,128)(2,1)S(1)}, bf16[512,512]{1,0:T(8,128)(2,1)S(1)}, u32[]{:S(2)}, u32[]{:S(2)}) collective-permute-start(bf16[512,512]{1,0:T(8,128)(2,1)S(1)} %slice.110), channel_id=1, source_target_pairs={{0,32},{32,64},{64,96},{96,0},{1,33},{33,65},{65,97},{97,1},{2,34}... | collective-permute-start | bytes 1572872 | tf_op jit(solution)/shard_map/ppermute | solution.py:13
  197.2 12.3 %collective-permute-start.47 = (bf16[512,512]{1,0:T(8,128)(2,1)S(1)}, bf16[512,512]{1,0:T(8,128)(2,1)S(1)}, u32[]{:S(2)}, u32[]{:S(2)}) collective-permute-start(bf16[512,512]{1,0:T(8,128)(2,1)S(1)} %slice.111), channel_id=1, source_target_pairs={{0,96},{32,0},{64,32},{96,64},{1,97},{33,1},{65,33},{97,65},{2,98}... | collective-permute-start | bytes 1572872 | tf_op jit(solution)/shard_map/ppermute | solution.py:13
  200.0 11.8 %collective-permute-start.48 = (bf16[128,2048]{1,0:T(8,128)(2,1)S(1)}, bf16[128,2048]{1,0:T(8,128)(2,1)S(1)}, u32[]{:S(2)}, u32[]{:S(2)}) collective-permute-start(bf16[128,2048]{1,0:T(8,128)(2,1)S(1)} %slice.113), channel_id=1, source_target_pairs={{0,4},{4,8},{8,12},{12,0},{1,5},{5,9},{9,13},{13,1},{2,6},{6,10},{... | collective-permute-start | bytes 1572872 | tf_op jit(solution)/shard_map/ppermute | solution.py:13
  200.1 12.2 %collective-permute-start.49 = (bf16[128,2048]{1,0:T(8,128)(2,1)S(1)}, bf16[128,2048]{1,0:T(8,128)(2,1)S(1)}, u32[]{:S(2)}, u32[]{:S(2)}) collective-permute-start(bf16[128,2048]{1,0:T(8,128)(2,1)S(1)} %slice.114), channel_id=1, source_target_pairs={{0,12},{4,0},{8,4},{12,8},{1,13},{5,1},{9,5},{13,9},{2,14},{6,2},{... | collective-permute-start | bytes 1572872 | tf_op jit(solution)/shard_map/ppermute | solution.py:13
  213.5 7.9 %collective-permute-start.50 = (f32[256,2048]{1,0:T(8,128)S(1)}, f32[256,2048]{1,0:T(8,128)S(1)}, u32[]{:S(2)}, u32[]{:S(2)}) collective-permute-start(f32[256,2048]{1,0:T(8,128)S(1)} %fusion.5), channel_id=1, source_target_pairs={{0,16},{16,0},{1,17},{17,1},{2,18},{18,2},{3,19},{19,3},{4,20},{20... | collective-permute-start | bytes 6291464 | tf_op jit(solution)/shard_map/ppermute | solution.py:13
where the time goes:
time: 223 us
  starting transfers between devices  102 us (46%)
  waiting for transfers between devices  86.5 us (39%)
  matrix products  20.8 us (9%)
  other arithmetic  10.7 us (5%)
  local copies, waits for them, and re-layouts  2.9 us (1%)
    ppermute x51, starting transfers between devices, shifted(): lax.ppermute(array, axis, [(i, (i + step) % size) for i in range(size)])  102 us
    ppermute x51, waiting for transfers between devices, shifted(): lax.ppermute(array, axis, [(i, (i + step) % size) for i in range(size)])  86.5 us
    dot_general x16, matrix products, matmul_rows(): lax.dot_general(left, right, (((0,), (0,)), ((), ())), preferred_element_...  7.62 us
    dot_general x1, matrix products, body(): own_part = jnp.dot(own_rows, weight, preferred_element_type=jnp.float32)  6.51 us
  transfers between devices with their start and end apart: 51, of which 22 were waited for; matrix products, arithmetic and copies ran while one was open for 9% of the time, Pallas kernels for 0%

commit v1 on v0

--- a/solution.py
+++ b/solution.py
@@ -34,8 +34,7 @@
     return [array] + [shifted(array, axis, step) for step in others]
 
 
-def in_place(pieces, axis, dim):
-    place = lax.axis_index(axis)
+def in_place(pieces, place, dim):
     size = pieces[0].shape[dim]
     shape = list(pieces[0].shape)
     shape[dim] = 4 * size
@@ -74,57 +73,54 @@
     own_rows = jnp.where(first, hidden_a, hidden_b)
     other_rows = jnp.where(first, hidden_b, hidden_a)
     own_rows, other_rows = lax.optimization_barrier((own_rows, other_rows))
-    passed = jnp.dot(other_rows, weight, preferred_element_type=jnp.float32).astype(jnp.bfloat16)
-    own_part = jnp.dot(own_rows, weight, preferred_element_type=jnp.float32)
-    passed, own_part = shifted(passed, "core", 1), lax.optimization_barrier(own_part)
+    chunks, half = 2, hidden_a.shape[0] // 2
+    project = lambda rows: jnp.dot(rows, weight, preferred_element_type=jnp.float32)
+    pieces = []
+    for chunk in range(chunks):
+        rows = slice(chunk * half, (chunk + 1) * half)
+        passed = shifted(project(other_rows[rows]).astype(jnp.bfloat16), "core", 1)
+        own_part = lax.optimization_barrier(project(own_rows[rows]))
+        made_here = made(
+            lambda step: part(own_part, chip + step, 4, 1)
+            + part(passed, chip + step, 4, 1).astype(jnp.float32)
+        )
+        made_here, own_rows, other_rows = lax.optimization_barrier(
+            (made_here, own_rows, other_rows)
+        )
+        pieces.append(made_here)
     mine_low, everyone = [], []
-    pieces = []
-    for chunk in range(2):
-        at = lambda step: 2 * ((chip + step) & 3) + chunk
-        pieces.append(
-            made(
-                lambda step: part(own_part, at(step), 8, 1)
-                + part(passed, at(step), 8, 1).astype(jnp.float32)
-            )
-        )
-    pieces = lax.optimization_barrier(pieces)
-    for chunk in range(2):
+    for chunk in range(chunks):
         total = summed(pieces[chunk], "x")
-        mine_low.append(total.astype(jnp.bfloat16))
-    for chunk in range(2):
-        everyone.append(jnp.concatenate(spread_over(mine_low[chunk], "crop")))
-    mine_low = jnp.concatenate(mine_low, axis=1)
+        mine_low.append(lax.optimization_barrier(total.astype(jnp.bfloat16)))
+    for chunk in range(chunks):
+        everyone += spread_over(mine_low[chunk], "crop")
+    mine_low = jnp.concatenate(mine_low)
     mine = mine_low.astype(jnp.float32)
     theirs = shifted(mine_low, "core", 1).astype(jnp.float32)
 
-    gram, rounded_all, col_means, spread = 0.0, [], [], []
-    rows = mine.shape[0]
-    for chunk in everyone:
-        chunk = chunk.astype(jnp.float32)
-        col_means.append(jnp.mean(chunk, axis=0))
-        centered = chunk - col_means[-1]
-        spread.append(jnp.sum(centered * centered, axis=0))
-        low = centered.astype(jnp.bfloat16)
-        rounded_all.append(low)
-        gram = gram + jnp.einsum("rf,bf->rb", low[:rows], low, preferred_element_type=jnp.float32)
-    col_means, spread = jnp.concatenate(col_means), jnp.concatenate(spread)
-    rounded_all = jnp.concatenate(rounded_all, axis=1)
+    everyone = jnp.concatenate(everyone).astype(jnp.float32)
+    col_means = jnp.mean(everyone, axis=0)
+    centered_all = everyone - col_means
+    spread = jnp.sum(centered_all * centered_all, axis=0)
+    rounded_all = centered_all.astype(jnp.bfloat16)
     deviation = jnp.sqrt(spread / (total_rows - 1.0) + epsilon)
     centered = mine - col_means
+    gram = jnp.einsum(
+        "rf,bf->rb", centered.astype(jnp.bfloat16), rounded_all, preferred_element_type=jnp.float32
+    )
 
     gram, hidden_a, hidden_b = lax.optimization_barrier((gram, hidden_a, hidden_b))
     features = rows_for_features(hidden_a, hidden_b)
-    half = rows // 2
     ways = (("x", chip, "tensor", gram[:half]), ("tensor", plane, "x", gram[half:]))
     sums = [
         summed(made(lambda step: part(g, at + step, 4, 0)), axis)
         for axis, at, _, g in ways
     ]
     sums = [summed(made(lambda step: s), then).astype(jnp.bfloat16) for s, (_, _, then, _) in zip(sums, ways)]
-    gram_low = jnp.concatenate(
-        [in_place(spread_over(s, axis), axis, 0) for s, (axis, _, _, _) in zip(sums, ways)]
-    )
-    gram_low, features = lax.optimization_barrier((gram_low, features))
+    gram_low = []
+    for s, (axis, at, _, _) in zip(sums, ways):
+        gram_low.append(in_place(spread_over(s, axis), at, 0))
+    gram_low, features = lax.optimization_barrier((jnp.concatenate(gram_low), features))
     products = jnp.dot(gram_low, rounded_all, preferred_element_type=jnp.float32)
 
     hinge_rate = jnp.where(deviation < 1.0, 25.0 / ((total_rows - 1.0) * deviation), 0.0)
@@ -141,7 +137,7 @@
     wanted = (shifted(other_view, "core", 1), own_view)
 
     tall = jnp.concatenate(spread_over(row_grads[:half], "crop"))
-    wide = in_place(spread_over(row_grads[half:], "x"), "x", 1)
+    wide = in_place(spread_over(row_grads[half:], "x"), chip, 1)
     tall_up, tall_down, tall_far = from_ring(tall, "x", 0)
     wide_up, wide_down, wide_far = from_ring(wide, "crop", 0)
     parts = []
@@ -152,7 +148,7 @@
         out = matmul_rows(far[0], wide) + matmul_rows(far[1], wide_up)
         out = out + matmul_rows(far[2], wide_down)
         talls = (tall, tall_up, tall_down, jnp.concatenate(tall_far))
-        out = out + in_place([block(array) for array in talls], "x", 1)
+        out = out + in_place([block(array) for array in talls], chip, 1)
         parts.append(out + matmul_rows(far[3], jnp.concatenate(wide_far)))
     return shifted(parts[0], "core", 1) + parts[1]
 

time: 223 us -> 226 us (1.013)
  waiting for transfers between devices: 86.5 us -> 106 us
  starting transfers between devices: 102 us -> 85 us
  other arithmetic: 10.7 us -> 8.39 us
    ppermute x51 -> x52, waiting for transfers between devices: 86.5 us -> 106 us  [shifted(): lax.ppermute(array, axis, [(i, (i + step) % size) for i in range(size)])]
    ppermute x51 -> x52, starting transfers between devices: 102 us -> 85 us  [shifted(): lax.ppermute(array, axis, [(i, (i + step) % size) for i in range(size)])]
    dot_general x4 -> x5, matrix products: 11.7 us -> 11.9 us  [the longest x4 10.6 us: body(): jnp.dot(rows, weight, preferred_element_type=jnp.float32)]
  transfers between devices with their start and end apart: 51 -> 52, of which waited for: 22 -> 27; matrix products, arithmetic and copies ran while one was open for 9% -> 8% of each run, Pallas kernels for 0% -> 0%
where the time goes in v1:
time: 226 us
  waiting for transfers between devices  106 us (47%)
  starting transfers between devices  85 us (38%)
  matrix products  20.9 us (9%)
  other arithmetic  8.39 us (4%)
  local copies, waits for them, and re-layouts  4.3 us (2%)
    ppermute x52, waiting for transfers between devices, shifted(): lax.ppermute(array, axis, [(i, (i + step) % size) for i in range(size)])  106 us
    ppermute x52, starting transfers between devices, shifted(): lax.ppermute(array, axis, [(i, (i + step) % size) for i in range(size)])  85 us
    dot_general x4, matrix products, body(): jnp.dot(rows, weight, preferred_element_type=jnp.float32)  10.6 us
    dot_general x16, matrix products, matmul_rows(): lax.dot_general(left, right, (((0,), (0,)), ((), ())), preferred_element_...  7.63 us
  transfers between devices with their start and end apart: 52, of which 27 were waited for; matrix products, arithmetic and copies ran while one was open for 8% of the time, Pallas kernels for 0%

profile of v1, /device:TPU:1, one launch (start us, length us, event | category | flops | bytes accessed | tf_op | source)
XLA Modules:
  0.0 225.8 jit_solution(8301928829319021091)
XLA Ops:
  0.0 1.8 broadcast_select_fusion
  2.9 1.3 convolution_convert_fusion.1
  4.2 1.5 collective-permute-start
  5.7 1.3 fusion.38
  7.0 1.1 collective-permute-done
  8.1 1.5 add_convert_fusion.7
  9.6 4.6 %convolution_convert_fusion = bf16[256,2048]{1,0:T(8,128)(2,1)} fusion(bf16[1024,2048]{1,0:T(8,128)(2,1)} %param.5, bf16[512,1024]{1,0:T(8,128)(2,1)S(1)} %copy-done.5), kind=kOutput, calls=%fused_computation.21 | convolution fusion | flops 1074266112 | bytes 5767168 | tf_op jit(solution)/shard_map/dot_general | solution.py:77
  14.6 1.3 collective-permute-start.1
  15.9 1.4 collective-permute-start.2
  17.3 1.6 collective-permute-start.3
  18.9 3.4 %fusion.35 = f32[256,2048]{1,0:T(8,128)S(1)} fusion(bf16[1024,2048]{1,0:T(8,128)(2,1)} %param.5, bf16[512,1024]{1,0:T(8,128)(2,1)S(1)} %copy-done.3), kind=kOutput, calls=%fused_computation.73 | convolution fusion | flops 1073741824 | bytes 6815744 | tf_op jit(solution)/shard_map/dot_general | solution.py:77
  22.4 1.2 collective-permute-done.1
  23.5 6.7 %collective-permute-done.3 = bf16[256,512]{1,0:T(8,128)(2,1)S(1)} collective-permute-done((bf16[256,512]{1,0:T(8,128)(2,1)S(1)}, bf16[256,512]{1,0:T(8,128)(2,1)S(1)}, u32[]{:S(2)}, u32[]{:S(2)}) %collective-permute-start.3) | collective-permute-done | bytes 262176 | tf_op jit(solution)/shard_map/ppermute | solution.py:13
  30.4 1.4 collective-permute-start.8
  31.8 1.5 collective-permute-start.9
  34.4 2.1 collective-permute-start.6
  36.5 2.2 collective-permute-done.8
  38.7 1.6 collective-permute-start.10
  40.3 1.9 collective-permute-done.5
  42.2 4.2 %collective-permute-done.7 = bf16[256,512]{1,0:T(8,128)(2,1)S(1)} collective-permute-done((bf16[256,512]{1,0:T(8,128)(2,1)S(1)}, bf16[256,512]{1,0:T(8,128)(2,1)S(1)}, u32[]{:S(2)}, u32[]{:S(2)}) %collective-permute-start.7) | collective-permute-done | bytes 262176 | tf_op jit(solution)/shard_map/ppermute | solution.py:13
  46.7 2.7 %collective-permute-start.12 = (bf16[256,512]{1,0:T(8,128)(2,1)S(1)}, bf16[256,512]{1,0:T(8,128)(2,1)S(1)}, u32[]{:S(2)}, u32[]{:S(2)}) collective-permute-start(bf16[256,512]{1,0:T(8,128)(2,1)S(1)} %add_convert_fusion.2), channel_id=1, source_target_pairs={{0,12},{4,0},{8,4},{12,8},{1,13},{5,1},{9,5},{13,9},{2,14},{6,2},{... | collective-permute-start | bytes 786440 | tf_op jit(solution)/shard_map/ppermute | solution.py:13
  49.7 4.2 %collective-permute-start.36 = (bf16[512,512]{1,0:T(8,128)(2,1)S(1)}, bf16[512,512]{1,0:T(8,128)(2,1)S(1)}, u32[]{:S(2)}, u32[]{:S(2)}) collective-permute-start(bf16[512,512]{1,0:T(8,128)(2,1)S(1)} %pad_maximum_fusion.3), channel_id=1, source_target_pairs={{0,16},{16,0},{1,17},{17,1},{2,18},{18,2},{3,19},{19,3},{4,20},{20... | collective-permute-start | bytes 1572872 | tf_op jit(solution)/shard_map/ppermute | solution.py:13
  53.9 2.0 collective-permute-done.12
  55.9 2.8 %collective-permute-done.13 = bf16[256,512]{1,0:T(8,128)(2,1)S(1)} collective-permute-done((bf16[256,512]{1,0:T(8,128)(2,1)S(1)}, bf16[256,512]{1,0:T(8,128)(2,1)S(1)}, u32[]{:S(2)}, u32[]{:S(2)}) %collective-permute-start.13) | collective-permute-done | bytes 262176 | tf_op jit(solution)/shard_map/ppermute | solution.py:13
  59.1 1.3 fusion.11
  63.6 2.0 collective-permute-start.15
  66.4 3.0 %collective-permute-done.14 = bf16[64,2048]{1,0:T(8,128)(2,1)S(1)} collective-permute-done((bf16[64,2048]{1,0:T(8,128)(2,1)S(1)}, bf16[64,2048]{1,0:T(8,128)(2,1)S(1)}, u32[]{:S(2)}, u32[]{:S(2)}) %collective-permute-start.14) | collective-permute-done | bytes 262176 | tf_op jit(solution)/shard_map/ppermute | solution.py:13
  69.4 1.5 collective-permute-start.23
  71.9 3.4 %collective-permute-start.24 = (bf16[64,2048]{1,0:T(8,128)(2,1)S(1)}, bf16[64,2048]{1,0:T(8,128)(2,1)S(1)}, u32[]{:S(2)}, u32[]{:S(2)}) collective-permute-start(bf16[64,2048]{1,0:T(8,128)(2,1)S(1)} %get-tuple-element.70), channel_id=1, source_target_pairs={{0,3},{1,0},{2,1},{3,2},{4,7},{5,4},{6,5},{7,6},{8,11},{9,8},{10,9... | collective-permute-start | bytes 786440 | tf_op jit(solution)/shard_map/ppermute | solution.py:13
  77.0 4.4 %collective-permute-done.24 = bf16[64,2048]{1,0:T(8,128)(2,1)S(1)} collective-permute-done((bf16[64,2048]{1,0:T(8,128)(2,1)S(1)}, bf16[64,2048]{1,0:T(8,128)(2,1)S(1)}, u32[]{:S(2)}, u32[]{:S(2)}) %collective-permute-start.24) | collective-permute-done | bytes 262176 | tf_op jit(solution)/shard_map/ppermute | solution.py:13
  81.5 3.1 %collective-permute-start.18 = (bf16[64,2048]{1,0:T(8,128)(2,1)S(1)}, bf16[64,2048]{1,0:T(8,128)(2,1)S(1)}, u32[]{:S(2)}, u32[]{:S(2)}) collective-permute-start(bf16[64,2048]{1,0:T(8,128)(2,1)S(1)} %fusion.46), channel_id=1, source_target_pairs={{0,3},{1,0},{2,1},{3,2},{4,7},{5,4},{6,5},{7,6},{8,11},{9,8},{10,9... | collective-permute-start | bytes 786440 | tf_op jit(solution)/shard_map/ppermute | solution.py:13
  84.7 3.3 %collective-permute-done.17 = bf16[64,2048]{1,0:T(8,128)(2,1)S(1)} collective-permute-done((bf16[64,2048]{1,0:T(8,128)(2,1)S(1)}, bf16[64,2048]{1,0:T(8,128)(2,1)S(1)}, u32[]{:S(2)}, u32[]{:S(2)}) %collective-permute-start.17) | collective-permute-done | bytes 262176 | tf_op jit(solution)/shard_map/ppermute | solution.py:13
  88.0 6.0 %collective-permute-done.18 = bf16[64,2048]{1,0:T(8,128)(2,1)S(1)} collective-permute-done((bf16[64,2048]{1,0:T(8,128)(2,1)S(1)}, bf16[64,2048]{1,0:T(8,128)(2,1)S(1)}, u32[]{:S(2)}, u32[]{:S(2)}) %collective-permute-start.18) | collective-permute-done | bytes 262176 | tf_op jit(solution)/shard_map/ppermute | solution.py:13
  94.0 2.9 %collective-permute-start.27 = (bf16[64,2048]{1,0:T(8,128)(2,1)S(1)}, bf16[64,2048]{1,0:T(8,128)(2,1)S(1)}, u32[]{:S(2)}, u32[]{:S(2)}) collective-permute-start(bf16[64,2048]{1,0:T(8,128)(2,1)S(1)} %fusion.47), channel_id=1, source_target_pairs={{0,96},{32,0},{64,32},{96,64},{1,97},{33,1},{65,33},{97,65},{2,98}... | collective-permute-start | bytes 786440 | tf_op jit(solution)/shard_map/ppermute | solution.py:13
  97.4 2.7 %collective-permute-start.33 = (bf16[2,512,256]{2,1,0:T(8,128)(2,1)S(1)}, bf16[2,512,256]{2,1,0:T(8,128)(2,1)S(1)}, u32[]{:S(2)}, u32[]{:S(2)}) collective-permute-start(bf16[2,512,256]{2,1,0:T(8,128)(2,1)S(1)} %get-tuple-element.64), channel_id=1, source_target_pairs={{0,12},{4,0},{8,4},{12,8},{1,13},{5,1},{9,5},{13,9},{2,14},{6,2},{... | collective-permute-start | bytes 1572872 | tf_op jit(solution)/shard_map/ppermute | solution.py:13
  100.1 3.0 %collective-permute-done.27 = bf16[64,2048]{1,0:T(8,128)(2,1)S(1)} collective-permute-done((bf16[64,2048]{1,0:T(8,128)(2,1)S(1)}, bf16[64,2048]{1,0:T(8,128)(2,1)S(1)}, u32[]{:S(2)}, u32[]{:S(2)}) %collective-permute-start.27) | collective-permute-done | bytes 262176 | tf_op jit(solution)/shard_map/ppermute | solution.py:13
  103.1 2.3 %collective-permute-done.28 = bf16[64,2048]{1,0:T(8,128)(2,1)S(1)} collective-permute-done((bf16[64,2048]{1,0:T(8,128)(2,1)S(1)}, bf16[64,2048]{1,0:T(8,128)(2,1)S(1)}, u32[]{:S(2)}, u32[]{:S(2)}) %collective-permute-start.28) | collective-permute-done | bytes 262176 | tf_op jit(solution)/shard_map/ppermute | solution.py:13
  105.4 1.1 collective-permute-start.21
  106.9 3.4 %collective-permute-done.20 = bf16[64,2048]{1,0:T(8,128)(2,1)S(1)} collective-permute-done((bf16[64,2048]{1,0:T(8,128)(2,1)S(1)}, bf16[64,2048]{1,0:T(8,128)(2,1)S(1)}, u32[]{:S(2)}, u32[]{:S(2)}) %collective-permute-start.20) | collective-permute-done | bytes 262176 | tf_op jit(solution)/shard_map/ppermute | solution.py:13
  110.3 5.2 %collective-permute-done.21 = bf16[64,2048]{1,0:T(8,128)(2,1)S(1)} collective-permute-done((bf16[64,2048]{1,0:T(8,128)(2,1)S(1)}, bf16[64,2048]{1,0:T(8,128)(2,1)S(1)}, u32[]{:S(2)}, u32[]{:S(2)}) %collective-permute-start.21) | collective-permute-done | bytes 262176 | tf_op jit(solution)/shard_map/ppermute | solution.py:13
  115.4 2.3 %collective-permute-start.30 = (bf16[64,2048]{1,0:T(8,128)(2,1)S(1)}, bf16[64,2048]{1,0:T(8,128)(2,1)S(1)}, u32[]{:S(2)}, u32[]{:S(2)}) collective-permute-start(bf16[64,2048]{1,0:T(8,128)(2,1)S(1)} %get-tuple-element.48), channel_id=1, source_target_pairs={{0,3},{1,0},{2,1},{3,2},{4,7},{5,4},{6,5},{7,6},{8,11},{9,8},{10,9... | collective-permute-start | bytes 786440 | tf_op jit(solution)/shard_map/ppermute | solution.py:13
  117.8 1.2 collective-permute-start.22
  119.0 2.1 collective-permute-done.30
  121.0 1.6 collective-permute-start.31
  122.7 4.6 %collective-permute-done.22 = bf16[64,2048]{1,0:T(8,128)(2,1)S(1)} collective-permute-done((bf16[64,2048]{1,0:T(8,128)(2,1)S(1)}, bf16[64,2048]{1,0:T(8,128)(2,1)S(1)}, u32[]{:S(2)}, u32[]{:S(2)}) %collective-permute-start.22) | collective-permute-done | bytes 262176 | tf_op jit(solution)/shard_map/ppermute | solution.py:13
  127.3 2.3 %collective-permute-start.34 = (bf16[2,512,256]{2,1,0:T(8,128)(2,1)S(1)}, bf16[2,512,256]{2,1,0:T(8,128)(2,1)S(1)}, u32[]{:S(2)}, u32[]{:S(2)}) collective-permute-start(bf16[2,512,256]{2,1,0:T(8,128)(2,1)S(1)} %get-tuple-element.61), channel_id=1, source_target_pairs={{0,8},{4,12},{8,0},{12,4},{1,9},{5,13},{9,1},{13,5},{2,10},{6,14},... | collective-permute-start | bytes 1572872 | tf_op jit(solution)/shard_map/ppermute | solution.py:13
  129.9 6.9 %collective-permute-done.34 = bf16[2,512,256]{2,1,0:T(8,128)(2,1)S(1)} collective-permute-done((bf16[2,512,256]{2,1,0:T(8,128)(2,1)S(1)}, bf16[2,512,256]{2,1,0:T(8,128)(2,1)S(1)}, u32[]{:S(2)}, u32[]{:S(2)}) %collective-permute-start.34) | collective-permute-done | bytes 524320 | tf_op jit(solution)/shard_map/ppermute | solution.py:13
  136.9 1.5 fusion.24
  138.5 1.3 collective-permute-start.37
  139.9 1.4 collective-permute-start.38
  141.6 2.4 %collective-permute-start.43 = (bf16[256,512]{1,0:T(8,128)(2,1)S(1)}, bf16[256,512]{1,0:T(8,128)(2,1)S(1)}, u32[]{:S(2)}, u32[]{:S(2)}) collective-permute-start(bf16[256,512]{1,0:T(8,128)(2,1)S(1)} %get-tuple-element.73), channel_id=1, source_target_pairs={{0,12},{4,0},{8,4},{12,8},{1,13},{5,1},{9,5},{13,9},{2,14},{6,2},{... | collective-permute-start | bytes 786440 | tf_op jit(solution)/shard_map/ppermute | solution.py:13
  144.0 1.2 collective-permute-start.44
  145.6 4.8 %collective-permute-done.42 = bf16[256,512]{1,0:T(8,128)(2,1)S(1)} collective-permute-done((bf16[256,512]{1,0:T(8,128)(2,1)S(1)}, bf16[256,512]{1,0:T(8,128)(2,1)S(1)}, u32[]{:S(2)}, u32[]{:S(2)}) %collective-permute-start.42) | collective-permute-done | bytes 262176 | tf_op jit(solution)/shard_map/ppermute | solution.py:13
  150.4 5.3 %collective-permute-done.43 = bf16[256,512]{1,0:T(8,128)(2,1)S(1)} collective-permute-done((bf16[256,512]{1,0:T(8,128)(2,1)S(1)}, bf16[256,512]{1,0:T(8,128)(2,1)S(1)}, u32[]{:S(2)}, u32[]{:S(2)}) %collective-permute-start.43) | collective-permute-done | bytes 262176 | tf_op jit(solution)/shard_map/ppermute | solution.py:13
  155.7 16.5 %collective-permute-start.35 = (bf16[4,512,256]{2,1,0:T(8,128)(2,1)S(1)}, bf16[4,512,256]{2,1,0:T(8,128)(2,1)S(1)}, u32[]{:S(2)}, u32[]{:S(2)}) collective-permute-start(bf16[4,512,256]{2,1,0:T(8,128)(2,1)S(1)} %get-tuple-element.60), channel_id=1, source_target_pairs={{0,16},{16,0},{1,17},{17,1},{2,18},{18,2},{3,19},{19,3},{4,20},{20... | collective-permute-start | bytes 3145736 | tf_op jit(solution)/shard_map/ppermute | solution.py:13
  172.3 2.7 %collective-permute-start.46 = (bf16[1024,512]{1,0:T(8,128)(2,1)S(1)}, bf16[1024,512]{1,0:T(8,128)(2,1)S(1)}, u32[]{:S(2)}, u32[]{:S(2)}) collective-permute-start(bf16[1024,512]{1,0:T(8,128)(2,1)S(1)} %pad_maximum_fusion.2), channel_id=1, source_target_pairs={{0,96},{32,0},{64,32},{96,64},{1,97},{33,1},{65,33},{97,65},{2,98}... | collective-permute-start | bytes 3145736 | tf_op jit(solution)/shard_map/ppermute | solution.py:13
  175.2 3.5 %collective-permute-start.41 = (bf16[256,2048]{1,0:T(8,128)(2,1)S(1)}, bf16[256,2048]{1,0:T(8,128)(2,1)S(1)}, u32[]{:S(2)}, u32[]{:S(2)}) collective-permute-start(bf16[256,2048]{1,0:T(8,128)(2,1)S(1)} %constant_dynamic-update-slice_fusion.12), channel_id=1, source_target_pairs={{0,12},{4,0},{8,4},{12,8},{1,13},{5,1},{9,5},{13,9},{2,14},{6,2},{... | collective-permute-start | bytes 3145736 | tf_op jit(solution)/shard_map/ppermute | solution.py:13
  180.2 19.7 %collective-permute-done.45 = bf16[1024,512]{1,0:T(8,128)(2,1)S(1)} collective-permute-done((bf16[1024,512]{1,0:T(8,128)(2,1)S(1)}, bf16[1024,512]{1,0:T(8,128)(2,1)S(1)}, u32[]{:S(2)}, u32[]{:S(2)}) %collective-permute-start.45) | collective-permute-done | bytes 1048608 | tf_op jit(solution)/shard_map/ppermute | solution.py:13
  200.0 2.7 %collective-permute-start.48 = (bf16[512,512]{1,0:T(8,128)(2,1)S(1)}, bf16[512,512]{1,0:T(8,128)(2,1)S(1)}, u32[]{:S(2)}, u32[]{:S(2)}) collective-permute-start(bf16[512,512]{1,0:T(8,128)(2,1)S(1)} %slice.117), channel_id=1, source_target_pairs={{0,96},{32,0},{64,32},{96,64},{1,97},{33,1},{65,33},{97,65},{2,98}... | collective-permute-start | bytes 1572872 | tf_op jit(solution)/shard_map/ppermute | solution.py:13
  202.9 2.7 %collective-permute-start.50 = (bf16[128,2048]{1,0:T(8,128)(2,1)S(1)}, bf16[128,2048]{1,0:T(8,128)(2,1)S(1)}, u32[]{:S(2)}, u32[]{:S(2)}) collective-permute-start(bf16[128,2048]{1,0:T(8,128)(2,1)S(1)} %slice.120), channel_id=1, source_target_pairs={{0,12},{4,0},{8,4},{12,8},{1,13},{5,1},{9,5},{13,9},{2,14},{6,2},{... | collective-permute-start | bytes 1572872 | tf_op jit(solution)/shard_map/ppermute | solution.py:13
  207.5 5.9 %collective-permute-done.47 = bf16[512,512]{1,0:T(8,128)(2,1)S(1)} collective-permute-done((bf16[512,512]{1,0:T(8,128)(2,1)S(1)}, bf16[512,512]{1,0:T(8,128)(2,1)S(1)}, u32[]{:S(2)}, u32[]{:S(2)}) %collective-permute-start.47) | collective-permute-done | bytes 524320 | tf_op jit(solution)/shard_map/ppermute | solution.py:13
  213.5 2.3 collective-permute-done.49
  217.4 3.0 %collective-permute-start.51 = (f32[256,2048]{1,0:T(8,128)S(1)}, f32[256,2048]{1,0:T(8,128)S(1)}, u32[]{:S(2)}, u32[]{:S(2)}) collective-permute-start(f32[256,2048]{1,0:T(8,128)S(1)} %fusion.8), channel_id=1, source_target_pairs={{0,16},{16,0},{1,17},{17,1},{2,18},{18,2},{3,19},{19,3},{4,20},{20... | collective-permute-start | bytes 6291464 | tf_op jit(solution)/shard_map/ppermute | solution.py:13
  224.2 1.6 add.209
  (132 shorter events, 21.8 us)
Async XLA Ops:
  0.0 2.9 %copy-start.6 = (bf16[1024,2048]{1,0:T(8,128)(2,1)S(1)}, bf16[1024,2048]{1,0:T(8,128)(2,1)}, u32[]{:S(2)}) copy-start(bf16[1024,2048]{1,0:T(8,128)(2,1)} %param.5) | copy-start | bytes 12582916
  1.8 2.4 %copy-start.4 = (bf16[512,1024]{1,0:T(8,128)(2,1)}, bf16[512,1024]{1,0:T(8,128)(2,1)S(1)}, u32[]{:S(2)}) copy-start(bf16[512,1024]{1,0:T(8,128)(2,1)S(1)} %get-tuple-element.32) | copy-start | bytes 3145732
  1.8 3.8 %copy-start.2 = (bf16[512,1024]{1,0:T(8,128)(2,1)}, bf16[512,1024]{1,0:T(8,128)(2,1)S(1)}, u32[]{:S(2)}) copy-start(bf16[512,1024]{1,0:T(8,128)(2,1)S(1)} %get-tuple-element.31) | copy-start | bytes 3145732
  4.2 3.9 %collective-permute-start = (bf16[256,2048]{1,0:T(8,128)(2,1)S(1)}, bf16[256,2048]{1,0:T(8,128)(2,1)}, u32[]{:S(2)}, u32[]{:S(2)}) collective-permute-start(bf16[256,2048]{1,0:T(8,128)(2,1)S(1)} %convolution_convert_fusion.1), channel_id=1, source_target_pairs={{0,16},{16,0},{1,17},{17,1},{2,18},{18,2},{3,19},{19,3},{4,20},{20... | collective-permute-start | bytes 3145736 | tf_op jit(solution)/shard_map/ppermute | solution.py:13
  7.0 2.7 %copy-start.5 = (bf16[512,1024]{1,0:T(8,128)(2,1)S(1)}, bf16[512,1024]{1,0:T(8,128)(2,1)}, u32[]{:S(2)}) copy-start(bf16[512,1024]{1,0:T(8,128)(2,1)} %copy-done.4) | copy-start | bytes 3145732
  9.6 9.3 %copy-start.3 = (bf16[512,1024]{1,0:T(8,128)(2,1)S(1)}, bf16[512,1024]{1,0:T(8,128)(2,1)}, u32[]{:S(2)}) copy-start(bf16[512,1024]{1,0:T(8,128)(2,1)} %copy-done.2) | copy-start | bytes 3145732
  14.2 19.1 %collective-permute-start.4 = (bf16[256,2048]{1,0:T(8,128)(2,1)}, bf16[256,2048]{1,0:T(8,128)(2,1)S(1)}, u32[]{:S(2)}, u32[]{:S(2)}) collective-permute-start(bf16[256,2048]{1,0:T(8,128)(2,1)} %convolution_convert_fusion), channel_id=1, source_target_pairs={{0,16},{16,0},{1,17},{17,1},{2,18},{18,2},{3,19},{19,3},{4,20},{20... | collective-permute-start | bytes 3145736 | tf_op jit(solution)/shard_map/ppermute | solution.py:13
  14.6 8.9 %collective-permute-start.1 = (bf16[256,512]{1,0:T(8,128)(2,1)S(1)}, bf16[256,512]{1,0:T(8,128)(2,1)S(1)}, u32[]{:S(2)}, u32[]{:S(2)}) collective-permute-start(bf16[256,512]{1,0:T(8,128)(2,1)S(1)} %get-tuple-element.28), channel_id=1, source_target_pairs={{0,32},{32,64},{64,96},{96,0},{1,33},{33,65},{65,97},{97,1},{2,34}... | collective-permute-start | bytes 786440 | tf_op jit(solution)/shard_map/ppermute | solution.py:13
  15.9 7.6 %collective-permute-start.2 = (bf16[256,512]{1,0:T(8,128)(2,1)S(1)}, bf16[256,512]{1,0:T(8,128)(2,1)S(1)}, u32[]{:S(2)}, u32[]{:S(2)}) collective-permute-start(bf16[256,512]{1,0:T(8,128)(2,1)S(1)} %get-tuple-element.29), channel_id=1, source_target_pairs={{0,96},{32,0},{64,32},{96,64},{1,97},{33,1},{65,33},{97,65},{2,98}... | collective-permute-start | bytes 786440 | tf_op jit(solution)/shard_map/ppermute | solution.py:13
  17.3 13.0 %collective-permute-start.3 = (bf16[256,512]{1,0:T(8,128)(2,1)S(1)}, bf16[256,512]{1,0:T(8,128)(2,1)S(1)}, u32[]{:S(2)}, u32[]{:S(2)}) collective-permute-start(bf16[256,512]{1,0:T(8,128)(2,1)S(1)} %get-tuple-element.30), channel_id=1, source_target_pairs={{0,64},{32,96},{64,0},{96,32},{1,65},{33,97},{65,1},{97,33},{2,66}... | collective-permute-start | bytes 786440 | tf_op jit(solution)/shard_map/ppermute | solution.py:13
  30.4 8.3 %collective-permute-start.8 = (bf16[256,512]{1,0:T(8,128)(2,1)S(1)}, bf16[256,512]{1,0:T(8,128)(2,1)S(1)}, u32[]{:S(2)}, u32[]{:S(2)}) collective-permute-start(bf16[256,512]{1,0:T(8,128)(2,1)S(1)} %add_convert_fusion.6), channel_id=1, source_target_pairs={{0,4},{4,8},{8,12},{12,0},{1,5},{5,9},{9,13},{13,1},{2,6},{6,10},{... | collective-permute-start | bytes 786440 | tf_op jit(solution)/shard_map/ppermute | solution.py:13
  31.8 8.5 %collective-permute-start.9 = (bf16[256,512]{1,0:T(8,128)(2,1)S(1)}, bf16[256,512]{1,0:T(8,128)(2,1)S(1)}, u32[]{:S(2)}, u32[]{:S(2)}) collective-permute-start(bf16[256,512]{1,0:T(8,128)(2,1)S(1)} %add_convert_fusion.6), channel_id=1, source_target_pairs={{0,12},{4,0},{8,4},{12,8},{1,13},{5,1},{9,5},{13,9},{2,14},{6,2},{... | collective-permute-start | bytes 786440 | tf_op jit(solution)/shard_map/ppermute | solution.py:13
  33.8 8.4 %collective-permute-start.5 = (bf16[256,512]{1,0:T(8,128)(2,1)S(1)}, bf16[256,512]{1,0:T(8,128)(2,1)S(1)}, u32[]{:S(2)}, u32[]{:S(2)}) collective-permute-start(bf16[256,512]{1,0:T(8,128)(2,1)S(1)} %get-tuple-element.34), channel_id=1, source_target_pairs={{0,32},{32,64},{64,96},{96,0},{1,33},{33,65},{65,97},{97,1},{2,34}... | collective-permute-start | bytes 786440 | tf_op jit(solution)/shard_map/ppermute | solution.py:13
  34.4 7.8 %collective-permute-start.6 = (bf16[256,512]{1,0:T(8,128)(2,1)S(1)}, bf16[256,512]{1,0:T(8,128)(2,1)S(1)}, u32[]{:S(2)}, u32[]{:S(2)}) collective-permute-start(bf16[256,512]{1,0:T(8,128)(2,1)S(1)} %get-tuple-element.35), channel_id=1, source_target_pairs={{0,96},{32,0},{64,32},{96,64},{1,97},{33,1},{65,33},{97,65},{2,98}... | collective-permute-start | bytes 786440 | tf_op jit(solution)/shard_map/ppermute | solution.py:13
  36.5 9.9 %collective-permute-start.7 = (bf16[256,512]{1,0:T(8,128)(2,1)S(1)}, bf16[256,512]{1,0:T(8,128)(2,1)S(1)}, u32[]{:S(2)}, u32[]{:S(2)}) collective-permute-start(bf16[256,512]{1,0:T(8,128)(2,1)S(1)} %get-tuple-element.36), channel_id=1, source_target_pairs={{0,64},{32,96},{64,0},{96,32},{1,65},{33,97},{65,1},{97,33},{2,66}... | collective-permute-start | bytes 786440 | tf_op jit(solution)/shard_map/ppermute | solution.py:13
  38.7 7.9 %collective-permute-start.10 = (bf16[256,512]{1,0:T(8,128)(2,1)S(1)}, bf16[256,512]{1,0:T(8,128)(2,1)S(1)}, u32[]{:S(2)}, u32[]{:S(2)}) collective-permute-start(bf16[256,512]{1,0:T(8,128)(2,1)S(1)} %add_convert_fusion.6), channel_id=1, source_target_pairs={{0,8},{4,12},{8,0},{12,4},{1,9},{5,13},{9,1},{13,5},{2,10},{6,14},... | collective-permute-start | bytes 786440 | tf_op jit(solution)/shard_map/ppermute | solution.py:13
  46.6 7.3 %collective-permute-start.11 = (bf16[256,512]{1,0:T(8,128)(2,1)S(1)}, bf16[256,512]{1,0:T(8,128)(2,1)S(1)}, u32[]{:S(2)}, u32[]{:S(2)}) collective-permute-start(bf16[256,512]{1,0:T(8,128)(2,1)S(1)} %add_convert_fusion.2), channel_id=1, source_target_pairs={{0,4},{4,8},{8,12},{12,0},{1,5},{5,9},{9,13},{13,1},{2,6},{6,10},{... | collective-permute-start | bytes 786440 | tf_op jit(solution)/shard_map/ppermute | solution.py:13
  46.7 9.2 %collective-permute-start.12 = (bf16[256,512]{1,0:T(8,128)(2,1)S(1)}, bf16[256,512]{1,0:T(8,128)(2,1)S(1)}, u32[]{:S(2)}, u32[]{:S(2)}) collective-permute-start(bf16[256,512]{1,0:T(8,128)(2,1)S(1)} %add_convert_fusion.2), channel_id=1, source_target_pairs={{0,12},{4,0},{8,4},{12,8},{1,13},{5,1},{9,5},{13,9},{2,14},{6,2},{... | collective-permute-start | bytes 786440 | tf_op jit(solution)/shard_map/ppermute | solution.py:13
  49.4 9.3 %collective-permute-start.13 = (bf16[256,512]{1,0:T(8,128)(2,1)S(1)}, bf16[256,512]{1,0:T(8,128)(2,1)S(1)}, u32[]{:S(2)}, u32[]{:S(2)}) collective-permute-start(bf16[256,512]{1,0:T(8,128)(2,1)S(1)} %add_convert_fusion.2), channel_id=1, source_target_pairs={{0,8},{4,12},{8,0},{12,4},{1,9},{5,13},{9,1},{13,5},{2,10},{6,14},... | collective-permute-start | bytes 786440 | tf_op jit(solution)/shard_map/ppermute | solution.py:13
  49.7 87.1 %collective-permute-start.36 = (bf16[512,512]{1,0:T(8,128)(2,1)S(1)}, bf16[512,512]{1,0:T(8,128)(2,1)S(1)}, u32[]{:S(2)}, u32[]{:S(2)}) collective-permute-start(bf16[512,512]{1,0:T(8,128)(2,1)S(1)} %pad_maximum_fusion.3), channel_id=1, source_target_pairs={{0,16},{16,0},{1,17},{17,1},{2,18},{18,2},{3,19},{19,3},{4,20},{20... | collective-permute-start | bytes 1572872 | tf_op jit(solution)/shard_map/ppermute | solution.py:13
  60.4 1.2 copy-start
  60.4 1.5 copy-start.1
  62.2 67.7 %collective-permute-start.32 = (bf16[2,512,256]{2,1,0:T(8,128)(2,1)S(1)}, bf16[2,512,256]{2,1,0:T(8,128)(2,1)S(1)}, u32[]{:S(2)}, u32[]{:S(2)}) collective-permute-start(bf16[2,512,256]{2,1,0:T(8,128)(2,1)S(1)} %get-tuple-element.63), channel_id=1, source_target_pairs={{0,4},{4,8},{8,12},{12,0},{1,5},{5,9},{9,13},{13,1},{2,6},{6,10},{... | collective-permute-start | bytes 1572872 | tf_op jit(solution)/shard_map/ppermute | solution.py:13
  62.9 6.5 %collective-permute-start.14 = (bf16[64,2048]{1,0:T(8,128)(2,1)S(1)}, bf16[64,2048]{1,0:T(8,128)(2,1)S(1)}, u32[]{:S(2)}, u32[]{:S(2)}) collective-permute-start(bf16[64,2048]{1,0:T(8,128)(2,1)S(1)} %get-tuple-element.65), channel_id=1, source_target_pairs={{0,32},{32,64},{64,96},{96,0},{1,33},{33,65},{65,97},{97,1},{2,34}... | collective-permute-start | bytes 786440 | tf_op jit(solution)/shard_map/ppermute | solution.py:13
  63.6 8.3 %collective-permute-start.15 = (bf16[64,2048]{1,0:T(8,128)(2,1)S(1)}, bf16[64,2048]{1,0:T(8,128)(2,1)S(1)}, u32[]{:S(2)}, u32[]{:S(2)}) collective-permute-start(bf16[64,2048]{1,0:T(8,128)(2,1)S(1)} %get-tuple-element.67), channel_id=1, source_target_pairs={{0,96},{32,0},{64,32},{96,64},{1,97},{33,1},{65,33},{97,65},{2,98}... | collective-permute-start | bytes 786440 | tf_op jit(solution)/shard_map/ppermute | solution.py:13
  65.6 9.7 %collective-permute-start.16 = (bf16[64,2048]{1,0:T(8,128)(2,1)S(1)}, bf16[64,2048]{1,0:T(8,128)(2,1)S(1)}, u32[]{:S(2)}, u32[]{:S(2)}) collective-permute-start(bf16[64,2048]{1,0:T(8,128)(2,1)S(1)} %get-tuple-element.66), channel_id=1, source_target_pairs={{0,64},{32,96},{64,0},{96,32},{1,65},{33,97},{65,1},{97,33},{2,66}... | collective-permute-start | bytes 786440 | tf_op jit(solution)/shard_map/ppermute | solution.py:13
  69.4 7.6 %collective-permute-start.23 = (bf16[64,2048]{1,0:T(8,128)(2,1)S(1)}, bf16[64,2048]{1,0:T(8,128)(2,1)S(1)}, u32[]{:S(2)}, u32[]{:S(2)}) collective-permute-start(bf16[64,2048]{1,0:T(8,128)(2,1)S(1)} %get-tuple-element.68), channel_id=1, source_target_pairs={{0,1},{1,2},{2,3},{3,0},{4,5},{5,6},{6,7},{7,4},{8,9},{9,10},{10,1... | collective-permute-start | bytes 786440 | tf_op jit(solution)/shard_map/ppermute | solution.py:13
  71.9 9.5 %collective-permute-start.24 = (bf16[64,2048]{1,0:T(8,128)(2,1)S(1)}, bf16[64,2048]{1,0:T(8,128)(2,1)S(1)}, u32[]{:S(2)}, u32[]{:S(2)}) collective-permute-start(bf16[64,2048]{1,0:T(8,128)(2,1)S(1)} %get-tuple-element.70), channel_id=1, source_target_pairs={{0,3},{1,0},{2,1},{3,2},{4,7},{5,4},{6,5},{7,6},{8,11},{9,8},{10,9... | collective-permute-start | bytes 786440 | tf_op jit(solution)/shard_map/ppermute | solution.py:13
  75.3 9.2 %collective-permute-start.25 = (bf16[64,2048]{1,0:T(8,128)(2,1)S(1)}, bf16[64,2048]{1,0:T(8,128)(2,1)S(1)}, u32[]{:S(2)}, u32[]{:S(2)}) collective-permute-start(bf16[64,2048]{1,0:T(8,128)(2,1)S(1)} %get-tuple-element.69), channel_id=1, source_target_pairs={{0,2},{1,3},{2,0},{3,1},{4,6},{5,7},{6,4},{7,5},{8,10},{9,11},{10,... | collective-permute-start | bytes 786440 | tf_op jit(solution)/shard_map/ppermute | solution.py:13
  77.0 11.0 %collective-permute-start.17 = (bf16[64,2048]{1,0:T(8,128)(2,1)S(1)}, bf16[64,2048]{1,0:T(8,128)(2,1)S(1)}, u32[]{:S(2)}, u32[]{:S(2)}) collective-permute-start(bf16[64,2048]{1,0:T(8,128)(2,1)S(1)} %fusion.46), channel_id=1, source_target_pairs={{0,1},{1,2},{2,3},{3,0},{4,5},{5,6},{6,7},{7,4},{8,9},{9,10},{10,1... | collective-permute-start | bytes 786440 | tf_op jit(solution)/shard_map/ppermute | solution.py:13
  81.5 12.6 %collective-permute-start.18 = (bf16[64,2048]{1,0:T(8,128)(2,1)S(1)}, bf16[64,2048]{1,0:T(8,128)(2,1)S(1)}, u32[]{:S(2)}, u32[]{:S(2)}) collective-permute-start(bf16[64,2048]{1,0:T(8,128)(2,1)S(1)} %fusion.46), channel_id=1, source_target_pairs={{0,3},{1,0},{2,1},{3,2},{4,7},{5,4},{6,5},{7,6},{8,11},{9,8},{10,9... | collective-permute-start | bytes 786440 | tf_op jit(solution)/shard_map/ppermute | solution.py:13
  84.6 12.4 %collective-permute-start.19 = (bf16[64,2048]{1,0:T(8,128)(2,1)S(1)}, bf16[64,2048]{1,0:T(8,128)(2,1)S(1)}, u32[]{:S(2)}, u32[]{:S(2)}) collective-permute-start(bf16[64,2048]{1,0:T(8,128)(2,1)S(1)} %fusion.46), channel_id=1, source_target_pairs={{0,2},{1,3},{2,0},{3,1},{4,6},{5,7},{6,4},{7,5},{8,10},{9,11},{10,... | collective-permute-start | bytes 786440 | tf_op jit(solution)/shard_map/ppermute | solution.py:13
  88.0 9.3 %collective-permute-start.26 = (bf16[64,2048]{1,0:T(8,128)(2,1)S(1)}, bf16[64,2048]{1,0:T(8,128)(2,1)S(1)}, u32[]{:S(2)}, u32[]{:S(2)}) collective-permute-start(bf16[64,2048]{1,0:T(8,128)(2,1)S(1)} %fusion.47), channel_id=1, source_target_pairs={{0,32},{32,64},{64,96},{96,0},{1,33},{33,65},{65,97},{97,1},{2,34}... | collective-permute-start | bytes 786440 | tf_op jit(solution)/shard_map/ppermute | solution.py:13
  94.0 9.0 %collective-permute-start.27 = (bf16[64,2048]{1,0:T(8,128)(2,1)S(1)}, bf16[64,2048]{1,0:T(8,128)(2,1)S(1)}, u32[]{:S(2)}, u32[]{:S(2)}) collective-permute-start(bf16[64,2048]{1,0:T(8,128)(2,1)S(1)} %fusion.47), channel_id=1, source_target_pairs={{0,96},{32,0},{64,32},{96,64},{1,97},{33,1},{65,33},{97,65},{2,98}... | collective-permute-start | bytes 786440 | tf_op jit(solution)/shard_map/ppermute | solution.py:13
  97.0 8.4 %collective-permute-start.28 = (bf16[64,2048]{1,0:T(8,128)(2,1)S(1)}, bf16[64,2048]{1,0:T(8,128)(2,1)S(1)}, u32[]{:S(2)}, u32[]{:S(2)}) collective-permute-start(bf16[64,2048]{1,0:T(8,128)(2,1)S(1)} %fusion.47), channel_id=1, source_target_pairs={{0,64},{32,96},{64,0},{96,32},{1,65},{33,97},{65,1},{97,33},{2,66}... | collective-permute-start | bytes 786440 | tf_op jit(solution)/shard_map/ppermute | solution.py:13
  97.4 32.6 %collective-permute-start.33 = (bf16[2,512,256]{2,1,0:T(8,128)(2,1)S(1)}, bf16[2,512,256]{2,1,0:T(8,128)(2,1)S(1)}, u32[]{:S(2)}, u32[]{:S(2)}) collective-permute-start(bf16[2,512,256]{2,1,0:T(8,128)(2,1)S(1)} %get-tuple-element.64), channel_id=1, source_target_pairs={{0,12},{4,0},{8,4},{12,8},{1,13},{5,1},{9,5},{13,9},{2,14},{6,2},{... | collective-permute-start | bytes 1572872 | tf_op jit(solution)/shard_map/ppermute | solution.py:13
  103.1 7.2 %collective-permute-start.20 = (bf16[64,2048]{1,0:T(8,128)(2,1)S(1)}, bf16[64,2048]{1,0:T(8,128)(2,1)S(1)}, u32[]{:S(2)}, u32[]{:S(2)}) collective-permute-start(bf16[64,2048]{1,0:T(8,128)(2,1)S(1)} %get-tuple-element.46), channel_id=1, source_target_pairs={{0,32},{32,64},{64,96},{96,0},{1,33},{33,65},{65,97},{97,1},{2,34}... | collective-permute-start | bytes 786440 | tf_op jit(solution)/shard_map/ppermute | solution.py:13
  105.4 10.1 %collective-permute-start.21 = (bf16[64,2048]{1,0:T(8,128)(2,1)S(1)}, bf16[64,2048]{1,0:T(8,128)(2,1)S(1)}, u32[]{:S(2)}, u32[]{:S(2)}) collective-permute-start(bf16[64,2048]{1,0:T(8,128)(2,1)S(1)} %get-tuple-element.46), channel_id=1, source_target_pairs={{0,96},{32,0},{64,32},{96,64},{1,97},{33,1},{65,33},{97,65},{2,98}... | collective-permute-start | bytes 786440 | tf_op jit(solution)/shard_map/ppermute | solution.py:13
  110.3 7.5 %collective-permute-start.29 = (bf16[64,2048]{1,0:T(8,128)(2,1)S(1)}, bf16[64,2048]{1,0:T(8,128)(2,1)S(1)}, u32[]{:S(2)}, u32[]{:S(2)}) collective-permute-start(bf16[64,2048]{1,0:T(8,128)(2,1)S(1)} %get-tuple-element.48), channel_id=1, source_target_pairs={{0,1},{1,2},{2,3},{3,0},{4,5},{5,6},{6,7},{7,4},{8,9},{9,10},{10,1... | collective-permute-start | bytes 786440 | tf_op jit(solution)/shard_map/ppermute | solution.py:13
  115.4 5.6 %collective-permute-start.30 = (bf16[64,2048]{1,0:T(8,128)(2,1)S(1)}, bf16[64,2048]{1,0:T(8,128)(2,1)S(1)}, u32[]{:S(2)}, u32[]{:S(2)}) collective-permute-start(bf16[64,2048]{1,0:T(8,128)(2,1)S(1)} %get-tuple-element.48), channel_id=1, source_target_pairs={{0,3},{1,0},{2,1},{3,2},{4,7},{5,4},{6,5},{7,6},{8,11},{9,8},{10,9... | collective-permute-start | bytes 786440 | tf_op jit(solution)/shard_map/ppermute | solution.py:13
  117.8 9.6 %collective-permute-start.22 = (bf16[64,2048]{1,0:T(8,128)(2,1)S(1)}, bf16[64,2048]{1,0:T(8,128)(2,1)S(1)}, u32[]{:S(2)}, u32[]{:S(2)}) collective-permute-start(bf16[64,2048]{1,0:T(8,128)(2,1)S(1)} %get-tuple-element.46), channel_id=1, source_target_pairs={{0,64},{32,96},{64,0},{96,32},{1,65},{33,97},{65,1},{97,33},{2,66}... | collective-permute-start | bytes 786440 | tf_op jit(solution)/shard_map/ppermute | solution.py:13
  121.0 8.6 %collective-permute-start.31 = (bf16[64,2048]{1,0:T(8,128)(2,1)S(1)}, bf16[64,2048]{1,0:T(8,128)(2,1)S(1)}, u32[]{:S(2)}, u32[]{:S(2)}) collective-permute-start(bf16[64,2048]{1,0:T(8,128)(2,1)S(1)} %get-tuple-element.48), channel_id=1, source_target_pairs={{0,2},{1,3},{2,0},{3,1},{4,6},{5,7},{6,4},{7,5},{8,10},{9,11},{10,... | collective-permute-start | bytes 786440 | tf_op jit(solution)/shard_map/ppermute | solution.py:13
  127.3 9.5 %collective-permute-start.34 = (bf16[2,512,256]{2,1,0:T(8,128)(2,1)S(1)}, bf16[2,512,256]{2,1,0:T(8,128)(2,1)S(1)}, u32[]{:S(2)}, u32[]{:S(2)}) collective-permute-start(bf16[2,512,256]{2,1,0:T(8,128)(2,1)S(1)} %get-tuple-element.61), channel_id=1, source_target_pairs={{0,8},{4,12},{8,0},{12,4},{1,9},{5,13},{9,1},{13,5},{2,10},{6,14},... | collective-permute-start | bytes 1572872 | tf_op jit(solution)/shard_map/ppermute | solution.py:13
  138.5 33.8 %collective-permute-start.37 = (bf16[256,512]{1,0:T(8,128)(2,1)S(1)}, bf16[256,512]{1,0:T(8,128)(2,1)S(1)}, u32[]{:S(2)}, u32[]{:S(2)}) collective-permute-start(bf16[256,512]{1,0:T(8,128)(2,1)S(1)} %get-tuple-element.75), channel_id=1, source_target_pairs={{0,32},{32,64},{64,96},{96,0},{1,33},{33,65},{65,97},{97,1},{2,34}... | collective-permute-start | bytes 786440 | tf_op jit(solution)/shard_map/ppermute | solution.py:13
  139.9 35.2 %collective-permute-start.38 = (bf16[256,512]{1,0:T(8,128)(2,1)S(1)}, bf16[256,512]{1,0:T(8,128)(2,1)S(1)}, u32[]{:S(2)}, u32[]{:S(2)}) collective-permute-start(bf16[256,512]{1,0:T(8,128)(2,1)S(1)} %get-tuple-element.75), channel_id=1, source_target_pairs={{0,96},{32,0},{64,32},{96,64},{1,97},{33,1},{65,33},{97,65},{2,98}... | collective-permute-start | bytes 786440 | tf_op jit(solution)/shard_map/ppermute | solution.py:13
  141.3 9.1 %collective-permute-start.42 = (bf16[256,512]{1,0:T(8,128)(2,1)S(1)}, bf16[256,512]{1,0:T(8,128)(2,1)S(1)}, u32[]{:S(2)}, u32[]{:S(2)}) collective-permute-start(bf16[256,512]{1,0:T(8,128)(2,1)S(1)} %get-tuple-element.73), channel_id=1, source_target_pairs={{0,4},{4,8},{8,12},{12,0},{1,5},{5,9},{9,13},{13,1},{2,6},{6,10},{... | collective-permute-start | bytes 786440 | tf_op jit(solution)/shard_map/ppermute | solution.py:13
  141.6 14.2 %collective-permute-start.43 = (bf16[256,512]{1,0:T(8,128)(2,1)S(1)}, bf16[256,512]{1,0:T(8,128)(2,1)S(1)}, u32[]{:S(2)}, u32[]{:S(2)}) collective-permute-start(bf16[256,512]{1,0:T(8,128)(2,1)S(1)} %get-tuple-element.73), channel_id=1, source_target_pairs={{0,12},{4,0},{8,4},{12,8},{1,13},{5,1},{9,5},{13,9},{2,14},{6,2},{... | collective-permute-start | bytes 786440 | tf_op jit(solution)/shard_map/ppermute | solution.py:13
  144.0 28.2 %collective-permute-start.44 = (bf16[256,512]{1,0:T(8,128)(2,1)S(1)}, bf16[256,512]{1,0:T(8,128)(2,1)S(1)}, u32[]{:S(2)}, u32[]{:S(2)}) collective-permute-start(bf16[256,512]{1,0:T(8,128)(2,1)S(1)} %get-tuple-element.73), channel_id=1, source_target_pairs={{0,8},{4,12},{8,0},{12,4},{1,9},{5,13},{9,1},{13,5},{2,10},{6,14},... | collective-permute-start | bytes 786440 | tf_op jit(solution)/shard_map/ppermute | solution.py:13
  150.4 24.7 %collective-permute-start.39 = (bf16[256,512]{1,0:T(8,128)(2,1)S(1)}, bf16[256,512]{1,0:T(8,128)(2,1)S(1)}, u32[]{:S(2)}, u32[]{:S(2)}) collective-permute-start(bf16[256,512]{1,0:T(8,128)(2,1)S(1)} %get-tuple-element.75), channel_id=1, source_target_pairs={{0,64},{32,96},{64,0},{96,32},{1,65},{33,97},{65,1},{97,33},{2,66}... | collective-permute-start | bytes 786440 | tf_op jit(solution)/shard_map/ppermute | solution.py:13
  155.7 23.7 %collective-permute-start.35 = (bf16[4,512,256]{2,1,0:T(8,128)(2,1)S(1)}, bf16[4,512,256]{2,1,0:T(8,128)(2,1)S(1)}, u32[]{:S(2)}, u32[]{:S(2)}) collective-permute-start(bf16[4,512,256]{2,1,0:T(8,128)(2,1)S(1)} %get-tuple-element.60), channel_id=1, source_target_pairs={{0,16},{16,0},{1,17},{17,1},{2,18},{18,2},{3,19},{19,3},{4,20},{20... | collective-permute-start | bytes 3145736 | tf_op jit(solution)/shard_map/ppermute | solution.py:13
  172.2 27.6 %collective-permute-start.45 = (bf16[1024,512]{1,0:T(8,128)(2,1)S(1)}, bf16[1024,512]{1,0:T(8,128)(2,1)S(1)}, u32[]{:S(2)}, u32[]{:S(2)}) collective-permute-start(bf16[1024,512]{1,0:T(8,128)(2,1)S(1)} %pad_maximum_fusion.2), channel_id=1, source_target_pairs={{0,32},{32,64},{64,96},{96,0},{1,33},{33,65},{65,97},{97,1},{2,34}... | collective-permute-start | bytes 3145736 | tf_op jit(solution)/shard_map/ppermute | solution.py:13
  172.3 27.6 %collective-permute-start.46 = (bf16[1024,512]{1,0:T(8,128)(2,1)S(1)}, bf16[1024,512]{1,0:T(8,128)(2,1)S(1)}, u32[]{:S(2)}, u32[]{:S(2)}) collective-permute-start(bf16[1024,512]{1,0:T(8,128)(2,1)S(1)} %pad_maximum_fusion.2), channel_id=1, source_target_pairs={{0,96},{32,0},{64,32},{96,64},{1,97},{33,1},{65,33},{97,65},{2,98}... | collective-permute-start | bytes 3145736 | tf_op jit(solution)/shard_map/ppermute | solution.py:13
  175.1 27.6 %collective-permute-start.40 = (bf16[256,2048]{1,0:T(8,128)(2,1)S(1)}, bf16[256,2048]{1,0:T(8,128)(2,1)S(1)}, u32[]{:S(2)}, u32[]{:S(2)}) collective-permute-start(bf16[256,2048]{1,0:T(8,128)(2,1)S(1)} %constant_dynamic-update-slice_fusion.12), channel_id=1, source_target_pairs={{0,4},{4,8},{8,12},{12,0},{1,5},{5,9},{9,13},{13,1},{2,6},{6,10},{... | collective-permute-start | bytes 3145736 | tf_op jit(solution)/shard_map/ppermute | solution.py:13
  175.2 27.7 %collective-permute-start.41 = (bf16[256,2048]{1,0:T(8,128)(2,1)S(1)}, bf16[256,2048]{1,0:T(8,128)(2,1)S(1)}, u32[]{:S(2)}, u32[]{:S(2)}) collective-permute-start(bf16[256,2048]{1,0:T(8,128)(2,1)S(1)} %constant_dynamic-update-slice_fusion.12), channel_id=1, source_target_pairs={{0,12},{4,0},{8,4},{12,8},{1,13},{5,1},{9,5},{13,9},{2,14},{6,2},{... | collective-permute-start | bytes 3145736 | tf_op jit(solution)/shard_map/ppermute | solution.py:13
  199.9 13.6 %collective-permute-start.47 = (bf16[512,512]{1,0:T(8,128)(2,1)S(1)}, bf16[512,512]{1,0:T(8,128)(2,1)S(1)}, u32[]{:S(2)}, u32[]{:S(2)}) collective-permute-start(bf16[512,512]{1,0:T(8,128)(2,1)S(1)} %slice.116), channel_id=1, source_target_pairs={{0,32},{32,64},{64,96},{96,0},{1,33},{33,65},{65,97},{97,1},{2,34}... | collective-permute-start | bytes 1572872 | tf_op jit(solution)/shard_map/ppermute | solution.py:13
  200.0 13.5 %collective-permute-start.48 = (bf16[512,512]{1,0:T(8,128)(2,1)S(1)}, bf16[512,512]{1,0:T(8,128)(2,1)S(1)}, u32[]{:S(2)}, u32[]{:S(2)}) collective-permute-start(bf16[512,512]{1,0:T(8,128)(2,1)S(1)} %slice.117), channel_id=1, source_target_pairs={{0,96},{32,0},{64,32},{96,64},{1,97},{33,1},{65,33},{97,65},{2,98}... | collective-permute-start | bytes 1572872 | tf_op jit(solution)/shard_map/ppermute | solution.py:13
  202.8 13.0 %collective-permute-start.49 = (bf16[128,2048]{1,0:T(8,128)(2,1)S(1)}, bf16[128,2048]{1,0:T(8,128)(2,1)S(1)}, u32[]{:S(2)}, u32[]{:S(2)}) collective-permute-start(bf16[128,2048]{1,0:T(8,128)(2,1)S(1)} %slice.119), channel_id=1, source_target_pairs={{0,4},{4,8},{8,12},{12,0},{1,5},{5,9},{9,13},{13,1},{2,6},{6,10},{... | collective-permute-start | bytes 1572872 | tf_op jit(solution)/shard_map/ppermute | solution.py:13
  202.9 13.4 %collective-permute-start.50 = (bf16[128,2048]{1,0:T(8,128)(2,1)S(1)}, bf16[128,2048]{1,0:T(8,128)(2,1)S(1)}, u32[]{:S(2)}, u32[]{:S(2)}) collective-permute-start(bf16[128,2048]{1,0:T(8,128)(2,1)S(1)} %slice.120), channel_id=1, source_target_pairs={{0,12},{4,0},{8,4},{12,8},{1,13},{5,1},{9,5},{13,9},{2,14},{6,2},{... | collective-permute-start | bytes 1572872 | tf_op jit(solution)/shard_map/ppermute | solution.py:13
  217.4 6.8 %collective-permute-start.51 = (f32[256,2048]{1,0:T(8,128)S(1)}, f32[256,2048]{1,0:T(8,128)S(1)}, u32[]{:S(2)}, u32[]{:S(2)}) collective-permute-start(f32[256,2048]{1,0:T(8,128)S(1)} %fusion.8), channel_id=1, source_target_pairs={{0,16},{16,0},{1,17},{17,1},{2,18},{18,2},{3,19},{19,3},{4,20},{20... | collective-permute-start | bytes 6291464 | tf_op jit(solution)/shard_map/ppermute | solution.py:13
